TPU v7x, 512 devices: a whole 4x4x16 slice. The times are simulated.
512 devices in a mesh: gx: 64 (over z, x), gy: 8 (over y, core).
Axes of the slice: x: 4, y: 4, z: 16, core: 2. Of those that a mesh axis runs over, the one named last changes fastest.
Arguments:
- vectors: bfloat16 [65536, 768], P(('gx', 'gy')), may hold values from -6 to 6
- list_ids: int32 [65536], P(('gx', 'gy')), may hold values from 0 to 4095, as said below
- old_order: int32 [4096], replicated, may hold values from 0 to 4095, each once
- new_order: int32 [4096], replicated, may hold values from 0 to 4095, as said below
- centroids: bfloat16 [4096, 768], P('gx', 'gy'), may hold values from -6 to 6
- rotation: bfloat16 [768, 768], replicated, may hold values from -0.21875 to 0.21875
- codebook: bfloat16 [96, 8, 256], P('gy'), may hold values from -8 to 8
Outputs:
- quant_error: float32 [65536, 96], P(('gx', 'gy'))
- list_error: float32 [4096, 96], P('gx', 'gy')
Inputs may be any that keep to these rules, and one draw needn't show every extreme that they name: `list_ids`: owner o holds the lists new_order[o * 64] to new_order[(o + 1) * 64 - 1]. Of the 128 vectors of one device, at most 5 name lists of one owner; in every draw some owner receives exactly 5 vectors from every device that shares its index of gy, and every device sends exactly 5 to some owner. `new_order`: each list once. `old_order`: each list once.
All inputs are finite; a program needn't handle non-finite values.
Results may differ from a plain program's by a relative error of at most 0.012.
Values may be sent and summed in bfloat16 or wider, within the bound.
A program may use at most 128 MiB of HBM per device.

v0:
```python
import jax
import jax.numpy as jnp
from jax import lax
from jax.sharding import Mesh
from jax.sharding import PartitionSpec as P

GX = ("gx_0", "gx_1")
GY = ("gy_0", "gy_1")
GX_GY = ("gx_0", "gx_1", "gy_0", "gy_1")


def gathered_by_axis(shard, axes, dim):
    if not axes:
        return shard
    nearer = lax.all_gather(shard, axes[-1], axis=dim, tiled=True)
    return gathered_by_axis(nearer, axes[:-1], dim)


def joined_along(pieces, dim):
    lengths = list(pieces.shape[1:])
    lengths[dim] *= pieces.shape[0]
    return jnp.moveaxis(pieces, 0, dim).reshape(lengths)


def copy_for_each(shard, axis):
    devices = lax.axis_size(axis)
    return lax.all_to_all(
        jnp.broadcast_to(shard[None], (devices, *shard.shape)), axis, 0, 0, tiled=True
    )


def collect(shard, axis, dim):
    return joined_along(copy_for_each(shard, axis), dim)


def all_blocks(shard, axes, order):
    pieces = shard[None]
    for k in order:
        pieces = lax.all_gather(pieces, axes[k], axis=0, tiled=True)
    current = [lax.axis_size(axes[k]) for k in reversed(order)]
    pieces = pieces.reshape(*current, *shard.shape)
    turned = sorted(range(len(order)), key=lambda place: order[len(order) - 1 - place])
    return pieces.transpose(*turned, *range(len(order), pieces.ndim)).reshape(-1, *shard.shape)


def gather_axes(shard, axes, order, dim):
    return joined_along(all_blocks(shard, axes, order), dim)


def of_everyone(shard, axis):
    return copy_for_each(shard, axis).sum(axis=0)


def packed_total(arrays, axis):
    ravelled, at, finished = (jnp.concatenate([a.reshape(-1) for a in arrays]), 0, [])
    so_far = of_everyone(ravelled, axis)
    for a in arrays:
        finished.append(so_far[at : at + a.size].reshape(a.shape))
        at += a.size
    return tuple(finished)


def subspace_errors(turned, codewords, code_norm):
    row_count = turned.shape[0]
    subspaces, sub_width, code_count = codewords.shape
    group_size = 8
    group_count = subspaces // group_size
    lowered = turned.astype(jnp.bfloat16).reshape(row_count, group_count, group_size, sub_width)
    lowered = jnp.moveaxis(lowered, 1, 0)
    squares = jnp.sum(
        (turned * turned).reshape(row_count, group_count, group_size, sub_width), axis=3
    )
    squares = jnp.moveaxis(squares, 1, 0)
    book_groups = codewords.reshape(group_count, group_size, sub_width, code_count)
    norm_groups = code_norm.reshape(group_count, group_size, code_count)

    def one_group(operands):
        lowered_part, square_part, book_part, norm_part = operands
        inner_terms = jnp.einsum(
            "rgd,gdk->rgk", lowered_part, book_part, preferred_element_type=jnp.float32
        )
        inner_terms = lax.optimization_barrier(inner_terms.astype(jnp.bfloat16)).astype(jnp.float32)
        distance = square_part[:, :, None] - 2.0 * inner_terms + norm_part[None, :, :]
        return jnp.min(distance, axis=2)

    nearest = lax.map(one_group, (lowered, squares, book_groups, norm_groups))
    return jnp.moveaxis(nearest, 0, 1).reshape(row_count, subspaces)


def on_device(vectors, list_ids, old_order, new_order, centroids, rotation, codebook):
    owners = lax.axis_size(GX)
    owner_index = lax.axis_index(GX)
    lists_own = centroids.shape[0]
    list_total = old_order.shape[0]
    rows_dev = vectors.shape[0]
    feature_width = vectors.shape[1]
    capacity = 5 * rows_dev // (2 * owners)
    own_lists = lax.dynamic_slice_in_dim(new_order, owner_index * lists_own, lists_own)
    select = (own_lists[:, None] == old_order[None, :]).astype(jnp.bfloat16)
    own_part = jnp.dot(
        select, gathered_by_axis(centroids, GX, 0), preferred_element_type=jnp.float32
    )
    own_centroids = collect(own_part.astype(jnp.bfloat16), GY, 1)
    rot_cent = jnp.dot(own_centroids, rotation, preferred_element_type=jnp.float32)
    padded_cent = jnp.concatenate([rot_cent, jnp.zeros((1, feature_width), jnp.float32)], axis=0)
    codewords = gather_axes(codebook, ("gy_0", "gy_1"), (0, 1), 0)
    code_float = codewords.astype(jnp.float32)
    code_norm = jnp.sum(code_float * code_float, axis=1)
    subspaces = codewords.shape[0]
    slot_of = (
        jnp.zeros((list_total,), jnp.int32)
        .at[new_order]
        .set(jnp.arange(list_total, dtype=jnp.int32))
    )
    new_slot = slot_of[list_ids]
    dest_owner = new_slot // lists_own
    local_list = new_slot % lists_own
    owner_hits = (dest_owner[:, None] == jnp.arange(owners, dtype=jnp.int32)[None, :]).astype(
        jnp.int32
    )
    before = jnp.cumsum(owner_hits, axis=0) - owner_hits
    position = jnp.sum(before * owner_hits, axis=1)
    target = dest_owner * capacity + position
    labels_flat = jnp.full((owners * capacity,), lists_own, jnp.int32).at[target].set(local_list)
    outgoing = jnp.zeros((owners * capacity, feature_width), jnp.bfloat16).at[target].set(vectors)
    incoming = lax.all_to_all(
        outgoing.reshape(owners, capacity, feature_width),
        GX,
        split_axis=0,
        concat_axis=0,
        tiled=True,
    )
    labels = lax.all_to_all(
        labels_flat.astype(jnp.bfloat16).reshape(owners, capacity),
        GX,
        split_axis=0,
        concat_axis=0,
        tiled=True,
    )
    turned = jnp.dot(
        incoming.reshape(-1, feature_width), rotation, preferred_element_type=jnp.float32
    )
    finish_turned = turned
    label_rows = labels.reshape(-1).astype(jnp.int32)
    finish_turned = finish_turned - jnp.take(padded_cent, label_rows, axis=0)
    errors = subspace_errors(finish_turned, codewords, code_norm)
    results = errors.reshape(labels.shape[0], labels.shape[1], subspaces)
    returned = lax.all_to_all(results, GX, split_axis=0, concat_axis=0, tiled=True)
    quant_error = returned.reshape(owners * capacity, subspaces)[target]
    label_rows = labels.reshape(-1).astype(jnp.int32)
    member = (label_rows[:, None] == jnp.arange(lists_own, dtype=jnp.int32)[None, :]).astype(
        jnp.float32
    )
    list_sums = jnp.einsum(
        "rl,rm->lm", member, results.reshape(-1, subspaces), precision=lax.Precision.HIGHEST
    )
    counts = jnp.sum(member, axis=0)
    list_sums, counts = packed_total((list_sums, counts), GY)
    average = list_sums / jnp.maximum(counts, 1.0)[:, None]
    own_columns = subspaces // lax.axis_size(GY)
    list_error = lax.dynamic_slice_in_dim(average, lax.axis_index(GY) * own_columns, own_columns, 1)
    return (quant_error, list_error)


def solution(mesh):
    split = Mesh(mesh.devices.reshape(16, 4, 4, 2), ("gx_0", "gx_1", "gy_0", "gy_1"))
    in_specs = (P(GX_GY, None), P(GX_GY), P(), P(), P(GX, GY), P(), P(GY, None, None))
    out_specs = (P(GX_GY, None), P(GX, GY))
    return jax.shard_map(
        on_device, mesh=split, in_specs=in_specs, out_specs=out_specs, check_vma=False
    )
```

profile of v0, /device:TPU:1, one launch (start us, length us, event | category | flops | bytes accessed | tf_op | source)
XLA Modules:
  0.0 236.4 jit_solution(8549061887895580433)
XLA Ops:
  0.7 0.8 compare_select_fusion
  2.1 15.5 %scatter_custom_fusion = s32[4096]{0:T(1024)S(1)} fusion(s32[4096]{0:T(1024)S(1)} %compare_select_fusion, s32[4096]{0:T(1024)S(1)} %iota.9, s32[]{:T(128)} %constant.56.clone.1), kind=kCustom, calls=%fused_computation.37 | custom fusion | bytes 16388 | tf_op jit(solution)/shard_map/scatter | solution.py:113
  17.7 1.1 gather_fusion
  19.3 1.0 scatter_custom_fusion.2
  20.3 0.8 all_to_all.25
  21.1 19.1 %all-to-all-start.1 = ((bf16[64,1,5]{2,1,0:T(2,128)(2,1)}), bf16[64,1,5]{2,1,0:T(2,128)(2,1)S(1)}, u32[]{:S(2)}, u32[]{:S(2)}) async-start(bf16[64,1,5]{2,1,0:T(2,128)(2,1)} %all_to_all.25), calls=%async_computation.1 | async-start | bytes 65536 | tf_op jit(solution)/shard_map/all_to_all | solution.py:133
  40.2 0.8 dynamic_slice.22
  41.0 10.2 %all_gather.12 = bf16[256,96]{1,0:T(8,128)(2,1)S(1)} all-gather(bf16[64,96]{1,0:T(8,128)(2,1)} %param.13), channel_id=1, replica_groups=mesh['gx_0'=16,'gx_1'=4,'gy_0'=4,'gy_1'=2] {'gx_1'}, dimensions={0}, use_global_device_ids=true | all-gather | bytes 61440 | tf_op jit(solution)/shard_map/all_gather | solution.py:15
  51.2 29.5 %all_gather.13 = bf16[4096,96]{1,0:T(8,128)(2,1)S(1)} all-gather(bf16[256,96]{1,0:T(8,128)(2,1)S(1)} %all_gather.12), channel_id=1, replica_groups=mesh['gx_0'=16,'gx_1'=4,'gy_0'=4,'gy_1'=2] {'gx_0'}, dimensions={0}, use_global_device_ids=true | all-gather | bytes 835584 | tf_op jit(solution)/shard_map/all_gather | solution.py:15
  81.7 14.0 %all-to-all-start.2 = ((bf16[8,64,96]{2,1,0:T(8,128)(2,1)}), bf16[8,64,96]{2,1,0:T(8,128)(2,1)S(1)}, u32[]{:S(2)}, u32[]{:S(2)}) async-start(bf16[8,64,96]{2,1,0:T(8,128)(2,1)} %broadcast_in_dim.63), calls=%async_computation.2 | async-start | bytes 262144 | tf_op jit(solution)/shard_map/all_to_all | solution.py:27
  95.6 1.7 scatter_custom_fusion.1
  97.3 1.1 reshape.159
  98.4 2.5 %all-to-all-done.2 = bf16[8,64,96]{2,1,0:T(8,128)(2,1)S(1)} async-done(((bf16[8,64,96]{2,1,0:T(8,128)(2,1)}), bf16[8,64,96]{2,1,0:T(8,128)(2,1)S(1)}, u32[]{:S(2)}, u32[]{:S(2)}) %all-to-all-start.2) | async-done | bytes 98336 | tf_op jit(solution)/shard_map/all_to_all | solution.py:27
  100.9 12.0 %all-to-all-start = ((bf16[64,5,768]{2,1,0:T(8,128)(2,1)}), bf16[64,5,768]{2,1,0:T(8,128)(2,1)S(1)}, u32[]{:S(2)}, u32[]{:S(2)}) async-start(bf16[64,5,768]{2,1,0:T(8,128)(2,1)} %reshape.159), calls=%async_computation | async-start | bytes 1572864 | tf_op jit(solution)/shard_map/all_to_all | solution.py:126
  112.9 9.8 %all-gather = bf16[48,8,256]{2,1,0:T(8,128)(2,1)S(1)} all-gather(bf16[12,8,256]{2,1,0:T(8,128)(2,1)S(1)} %copy-done.2), channel_id=2, replica_groups=mesh['gx_0'=16,'gx_1'=4,'gy_0'=4,'gy_1'=2] {'gy_0'}, dimensions={0}, use_global_device_ids=true | all-gather | bytes 245760 | tf_op jit(solution)/shard_map/all_gather | solution.py:39
  122.7 5.1 %all_gather.15 = bf16[8,12,8,256]{3,2,1,0:T(8,128)(2,1)S(1)} all-gather(bf16[4,12,8,256]{3,2,1,0:T(8,128)(2,1)S(1)} %bitcast.69), channel_id=1, replica_groups=mesh['gx_0'=16,'gx_1'=4,'gy_0'=4,'gy_1'=2] {'gy_1'}, dimensions={0}, use_global_device_ids=true | all-gather | bytes 589824 | tf_op jit(solution)/shard_map/all_gather | solution.py:39
  127.8 0.8 copy.44
  130.7 1.9 gather_fusion.1
  132.6 20.8 %all-to-all-done = bf16[64,5,768]{2,1,0:T(8,128)(2,1)S(1)} async-done(((bf16[64,5,768]{2,1,0:T(8,128)(2,1)}), bf16[64,5,768]{2,1,0:T(8,128)(2,1)S(1)}, u32[]{:S(2)}, u32[]{:S(2)}) %all-to-all-start) | async-done | bytes 491552 | tf_op jit(solution)/shard_map/all_to_all | solution.py:126
  153.5 1.0 reshape.160
  154.4 2.4 %fusion.21 = (bf16[320,768]{1,0:T(8,128)(2,1)}, f32[320,768]{1,0:T(8,128)S(1)}) fusion(f32[320,768]{1,0:T(8,128)S(1)} %gather_fusion.1, pred[320]{0:T(512)(128)(4,1)S(1)} %compare_and_fusion, bf16[320,768]{1,0:T(8,128)(2,1)} %reshape.160, bf16[768,768]{1,0:T(8,128)(2,1)S(1)} %copy-done), kind=kOutput, calls=%fused_computation.63 | convolution fusion | flops 378470400 | bytes 4129088 | tf_op jit(solution)/shard_map/dot_general | solution.py:140
  157.5 0.7 copy-done.1
  158.5 39.3 %while.10 = (s32[]{:T(128)}, f32[12,320,8]{1,2,0:T(8,128)S(1)}, f32[12,320,8]{1,2,0:T(8,128)S(1)}, bf16[12,8,8,256]{3,2,1,0:T(8,128)(2,1)}, bf16[12,320,8,8]{1,3...) while((s32[]{:T(128)}, f32[12,320,8]{1,2,0:T(8,128)S(1)}, f32[12,320,8]{1,2,0:T(8,128)S(1)}, ...), condition=%wide.region_9.10_spmd, body=%wide.region_7.9_spmd.sunk | while | flops 14415362 | bytes 2794585 | solution.py:86
  158.6 1.3 fusion.33
  160.6 1.2 add_reduce_fusion.2
  161.8 1.3 fusion.33
  163.2 0.7 dynamic-slice_bitcast_fusion.4
  163.9 1.2 add_reduce_fusion.2
  165.1 1.3 fusion.33
  167.2 1.2 add_reduce_fusion.2
  168.4 1.3 fusion.33
  169.7 0.7 dynamic-slice_bitcast_fusion.4
  170.4 1.2 add_reduce_fusion.2
  171.7 1.3 fusion.33
  173.0 0.7 dynamic-slice_bitcast_fusion.4
  173.7 1.2 add_reduce_fusion.2
  174.9 1.3 fusion.33
  176.3 0.7 dynamic-slice_bitcast_fusion.4
  177.0 1.2 add_reduce_fusion.2
  178.2 1.3 fusion.33
  179.5 0.7 dynamic-slice_bitcast_fusion.4
  180.2 1.2 add_reduce_fusion.2
  181.5 1.3 fusion.33
  182.8 0.7 dynamic-slice_bitcast_fusion.4
  183.5 1.2 add_reduce_fusion.2
  184.7 1.3 fusion.33
  186.1 0.7 dynamic-slice_bitcast_fusion.4
  186.8 1.2 add_reduce_fusion.2
  188.0 1.3 fusion.33
  189.4 0.7 dynamic-slice_bitcast_fusion.4
  190.1 1.2 add_reduce_fusion.2
  191.3 1.3 fusion.33
  193.3 1.2 add_reduce_fusion.2
  194.6 1.3 fusion.33
  196.6 1.2 add_reduce_fusion.2
  198.2 0.8 broadcast_in_dim.66
  198.9 7.7 %all-to-all-start.4 = ((f32[8,1,6208]{2,1,0:T(1,128)}), f32[8,1,6208]{2,1,0:T(1,128)S(1)}, u32[]{:S(2)}, u32[]{:S(2)}) async-start(f32[8,1,6208]{2,1,0:T(1,128)} %broadcast_in_dim.66), calls=%async_computation.4 | async-start | bytes 401408 | tf_op jit(solution)/shard_map/all_to_all | solution.py:27
  206.6 2.8 %copy.47 = f32[320,12,8]{2,1,0:T(8,128)} copy(f32[320,12,8]{0,2,1:T(8,128)S(1)} %bitcast.70) | data formatting | bytes 245760 | tf_op jit(solution)/shard_map/transpose | solution.py:87
  209.4 2.6 %reshape_reshape.4 = f32[64,5,96]{2,1,0:T(8,128)S(1)} reshape(f32[320,12,8]{2,1,0:T(8,128)} %copy.47) | data formatting | bytes 245760 | tf_op jit(solution)/shard_map/reshape;reshape | solution.py:147
  212.0 0.9 reshape.239
  212.9 5.6 %all-to-all-start.3 = ((f32[64,1,480]{2,1,0:T(1,128)}), f32[64,1,480]{2,1,0:T(1,128)S(1)}, u32[]{:S(2)}, u32[]{:S(2)}) async-start(f32[64,1,480]{2,1,0:T(1,128)} %reshape.239), calls=%async_computation.3 | async-start | bytes 262144 | tf_op jit(solution)/shard_map/all_to_all | solution.py:148
  219.5 14.0 %all-to-all-done.3 = f32[64,1,480]{2,1,0:T(1,128)S(1)} async-done(((f32[64,1,480]{2,1,0:T(1,128)}), f32[64,1,480]{2,1,0:T(1,128)S(1)}, u32[]{:S(2)}, u32[]{:S(2)}) %all-to-all-start.3) | async-done | bytes 122912 | tf_op jit(solution)/shard_map/all_to_all | solution.py:148
  234.0 1.0 reduce.10
  235.7 0.7 copy.49
  (81 shorter events, 10.8 us)
Async XLA Ops:
  0.6 129.7 %copy-start = (bf16[768,768]{1,0:T(8,128)(2,1)S(1)}, bf16[768,768]{1,0:T(8,128)(2,1)}, u32[]{:S(2)}) copy-start(bf16[768,768]{1,0:T(8,128)(2,1)} %param.14) | copy-start | bytes 3538948
  0.6 80.0 %copy-start.3 = (s32[4096]{0:T(1024)S(1)}, s32[4096]{0:T(1024)}, u32[]{:S(2)}) copy-start(s32[4096]{0:T(1024)} %param.11) | copy-start | bytes 49156
  21.1 59.9 %all-to-all-start.1 = ((bf16[64,1,5]{2,1,0:T(2,128)(2,1)}), bf16[64,1,5]{2,1,0:T(2,128)(2,1)S(1)}, u32[]{:S(2)}, u32[]{:S(2)}) async-start(bf16[64,1,5]{2,1,0:T(2,128)(2,1)} %all_to_all.25), calls=%async_computation.1 | async-start | bytes 65536 | tf_op jit(solution)/shard_map/all_to_all | solution.py:133
  81.7 19.2 %all-to-all-start.2 = ((bf16[8,64,96]{2,1,0:T(8,128)(2,1)}), bf16[8,64,96]{2,1,0:T(8,128)(2,1)S(1)}, u32[]{:S(2)}, u32[]{:S(2)}) async-start(bf16[8,64,96]{2,1,0:T(8,128)(2,1)} %broadcast_in_dim.63), calls=%async_computation.2 | async-start | bytes 262144 | tf_op jit(solution)/shard_map/all_to_all | solution.py:27
  97.3 15.6 %copy-start.2 = (bf16[12,8,256]{2,1,0:T(8,128)(2,1)S(1)}, bf16[12,8,256]{2,1,0:T(8,128)(2,1)}, u32[]{:S(2)}) copy-start(bf16[12,8,256]{2,1,0:T(8,128)(2,1)} %param.15) | copy-start | bytes 147460
  100.9 52.6 %all-to-all-start = ((bf16[64,5,768]{2,1,0:T(8,128)(2,1)}), bf16[64,5,768]{2,1,0:T(8,128)(2,1)S(1)}, u32[]{:S(2)}, u32[]{:S(2)}) async-start(bf16[64,5,768]{2,1,0:T(8,128)(2,1)} %reshape.159), calls=%async_computation | async-start | bytes 1572864 | tf_op jit(solution)/shard_map/all_to_all | solution.py:126
  157.2 1.0 copy-start.1
  198.9 13.9 %all-to-all-start.4 = ((f32[8,1,6208]{2,1,0:T(1,128)}), f32[8,1,6208]{2,1,0:T(1,128)S(1)}, u32[]{:S(2)}, u32[]{:S(2)}) async-start(f32[8,1,6208]{2,1,0:T(1,128)} %broadcast_in_dim.66), calls=%async_computation.4 | async-start | bytes 401408 | tf_op jit(solution)/shard_map/all_to_all | solution.py:27
  212.9 20.6 %all-to-all-start.3 = ((f32[64,1,480]{2,1,0:T(1,128)}), f32[64,1,480]{2,1,0:T(1,128)S(1)}, u32[]{:S(2)}, u32[]{:S(2)}) async-start(f32[64,1,480]{2,1,0:T(1,128)} %reshape.239), calls=%async_computation.3 | async-start | bytes 262144 | tf_op jit(solution)/shard_map/all_to_all | solution.py:148
where the time goes:
time: 241 us; the launch traced here: 236 us
  starting transfers between devices  58.3 us (24%)
  blocking collectives  54.6 us (23%)
  local copies, waits for them, and re-layouts  47.4 us (20%)
  waiting for transfers between devices  37.3 us (15%)
  matrix products  19.1 us (8%)
  other arithmetic  18.2 us (8%)
    all_gather x2, blocking collectives, gathered_by_axis(): nearer = lax.all_gather(shard, axes[-1], axis=dim, tiled=True)  39.7 us
    all_to_all x2, starting transfers between devices, copy_for_each(): lax.all_to_all(jnp.broadcast_to(shard[None], (devices, *shard.shape)), ax...  21.7 us
    all_to_all x1, waiting for transfers between devices, on_device(): lax.all_to_all(outgoing.reshape(owners, capacity, feature_width), GX, spl...  20.8 us
    all_to_all x1, starting transfers between devices, on_device(): lax.all_to_all(labels_flat.astype(jnp.bfloat16).reshape(owners, capacity)...  19.1 us
    dot_general x12, matrix products, one_group(): jnp.einsum('rgd,gdk->rgk', lowered_part, book_part, preferred_element_typ...  15.8 us
    scatter x1, local copies, waits for them, and re-layouts, on_device(): slot_of = jnp.zeros((list_total,), jnp.int32).at[new_order].set(jnp.arang...  15.5 us
    all_gather x2, blocking collectives, all_blocks(): pieces = lax.all_gather(pieces, axes[k], axis=0, tiled=True)  15 us
    reduce_min x12, other arithmetic, one_group(): return jnp.min(distance, axis=2)  14.3 us
  transfers between devices with their start and end apart: 5, of which 3 were waited for; matrix products, arithmetic and copies ran while one was open for 7% of the time, Pallas kernels for 0%

commit v1 on v0

v1 whole, which is shorter than its diff:
```python
import jax
import jax.numpy as jnp
from jax import lax
from jax.experimental import pallas as pl
from jax.experimental.pallas import tpu as pltpu
from jax.sharding import PartitionSpec as P

MESH = pl.DeviceIdType.MESH
F32 = jnp.float32
BF16 = jnp.bfloat16

NZ, NX, NG = 16, 4, 8
NP = NX * NG
OWN = 64
FEAT = 96
SUB = 12
ROWS = 128
CODES = 256
HOP = 4
NEAR = [4, -4, 1, -1, 2, -2, 3, -3]
FAR = [5, -5, 6, -6, 7, -7, 8]


def kernel(
    v_hbm, ids_hbm, old_hbm, new_hbm, c_hbm, r_hbm, cb_hbm,
    q_hbm, le_hbm,
    v, ids, old, new, cg, rot, cb,
    slot_out, slots, scol, y, book, wt, acc, wout, win, vr,
    qmin, tt, qt, eout, ein, zrow, bt, lm, pout, pin, qout, lout,
    in_sem, zs_sem, xs_sem, ag_sem, cbs_sem, cb_sem, sls_sem, sl_sem,
    ws_sem, w_sem, es_sem, e_sem, ps_sem, p_sem, out_sem,
):
    gx, g = lax.axis_index("gx"), lax.axis_index("gy")
    z, x = gx // NX, gx % NX
    p_me = x * NG + g

    def at_z(off):
        return lax.rem(z + (off + NZ), NZ)

    def plane_dev(p):
        return (z * NX + p // NG, p % NG)

    loads = [
        pltpu.make_async_copy(c_hbm, cg.at[gx], in_sem.at[0]),
        pltpu.make_async_copy(ids_hbm, ids, in_sem.at[1]),
        pltpu.make_async_copy(old_hbm, old, in_sem.at[2]),
        pltpu.make_async_copy(new_hbm, new, in_sem.at[3]),
        pltpu.make_async_copy(cb_hbm, cb.at[g], in_sem.at[4]),
        pltpu.make_async_copy(v_hbm, v, in_sem.at[5]),
        pltpu.make_async_copy(r_hbm, rot, in_sem.at[6]),
    ]
    for one in loads:
        one.start()

    barrier = pltpu.get_barrier_semaphore()
    for off in NEAR:
        pl.semaphore_signal(barrier, inc=1, device_id=(at_z(off) * NX + x, g), device_id_type=MESH)

    def greet(d, carry):
        pl.semaphore_signal(
            barrier, inc=1, device_id=plane_dev(lax.rem(p_me + d, NP)), device_id_type=MESH
        )
        return carry

    lax.fori_loop(1, NP, greet, 0)

    for k in (1, 2, 3):
        loads[k].wait()
    lane = lax.broadcasted_iota(jnp.int32, (ROWS, 128), 1)
    lane_f = lane.astype(F32)
    id_col = jnp.broadcast_to(ids[...].astype(F32), (ROWS, 128)).T

    def find(order, row):
        total = jnp.zeros((ROWS, 128), F32)
        for k in range(32):
            entry = jnp.broadcast_to(order[k : k + 1, :].astype(F32), (ROWS, 128))
            total = total + jnp.where(id_col == entry, lane_f + float(128 * k), 0.0)
        slot_out[row : row + 1, :] = jnp.sum(total.T, axis=0, keepdims=True)

    slot_out[...] = jnp.zeros((8, 128), F32)
    find(old, 0)
    find(new, 1)

    loads[0].wait()
    loads[4].wait()
    pl.semaphore_wait(barrier, len(NEAR) + NP - 1)

    def z_copy(block_z, to_off, k):
        block = block_z * NX + x
        return pltpu.make_async_remote_copy(
            src_ref=cg.at[block], dst_ref=cg.at[block],
            send_sem=zs_sem.at[k], recv_sem=ag_sem.at[block],
            device_id=(at_z(to_off) * NX + x, g), device_id_type=MESH,
        )

    def x_copy(block_z, d):
        block = block_z * NX + x
        return pltpu.make_async_remote_copy(
            src_ref=cg.at[block], dst_ref=cg.at[block],
            send_sem=xs_sem.at[block_z * NX + d], recv_sem=ag_sem.at[block],
            device_id=(z * NX + lax.rem(x + d, NX), g), device_id_type=MESH,
        )

    def got(block):
        pltpu.make_async_remote_copy(
            src_ref=cg.at[block], dst_ref=cg.at[block],
            send_sem=zs_sem.at[0], recv_sem=ag_sem.at[block],
            device_id=(gx, g), device_id_type=MESH,
        ).wait_recv()

    sent = []
    for k, off in enumerate(NEAR):
        sent.append(z_copy(z, off, k))
        sent[-1].start()
    for d in (1, 3, 2):
        x_copy(z, d).start()

    def slot_copy(d):
        return pltpu.make_async_remote_copy(
            src_ref=slot_out, dst_ref=slots.at[p_me],
            send_sem=sls_sem.at[d], recv_sem=sl_sem.at[p_me],
            device_id=plane_dev(lax.rem(p_me + d, NP)), device_id_type=MESH,
        )

    def send_slots(d, carry):
        slot_copy(d).start()
        return carry

    lax.fori_loop(1, NP, send_slots, 0)
    slots[p_me] = slot_out[...]

    def book_copy(d):
        return pltpu.make_async_remote_copy(
            src_ref=cb.at[g], dst_ref=cb.at[g],
            send_sem=cbs_sem.at[d], recv_sem=cb_sem.at[g],
            device_id=(gx, lax.rem(g + d, NG)), device_id_type=MESH,
        )

    for d in range(1, NG):
        book_copy(d).start()

    loads[5].wait()
    loads[6].wait()
    vr[...] = jnp.dot(v[...], rot[...], preferred_element_type=F32)

    for off in NEAR[2:]:
        got(at_z(off) * NX + x)
        for d in (1, 3, 2):
            x_copy(at_z(off), d).start()
    k = len(NEAR)
    for off in NEAR[:2]:
        got(at_z(off) * NX + x)
        step = -1 if off > 0 else 1
        for far in range(HOP if off > 0 else HOP - 1, 0, -1):
            sent.append(z_copy(at_z(off), step * far, k))
            sent[-1].start()
            k += 1
    for off in NEAR[:2]:
        for d in (1, 3, 2):
            x_copy(at_z(off), d).start()

    y[...] = jnp.zeros_like(y)
    wt[...] = jnp.zeros_like(wt)
    for q in range(NG // 2):
        for h in range(2):
            wt[q, h * 128 + FEAT : (h + 1) * 128, h * 128 : (h + 1) * 128] = jnp.ones((32, 128), BF16)

    def book_got(d):
        other = lax.rem(g + d, NG)
        pltpu.make_async_remote_copy(
            src_ref=cb.at[other], dst_ref=cb.at[other],
            send_sem=cbs_sem.at[0], recv_sem=cb_sem.at[other],
            device_id=(gx, g), device_id_type=MESH,
        ).wait_recv()

    lane_row = lax.broadcasted_iota(jnp.int32, (1, 128), 1)
    member = jnp.where(lane_row < FEAT, lane_row // 8, lax.rem(lane_row - FEAT, 16))

    for d in range(1, NG):
        book_got(d)

    def build_book(q, carry):
        for h in range(2):
            words = cb[2 * q + h].astype(F32)
            norm = jnp.sum(words * words, axis=1)
            high = norm.astype(BF16).astype(F32)
            y[0:FEAT, :] = -2.0 * words.reshape(FEAT, CODES)
            y[FEAT : FEAT + SUB, :] = high
            y[FEAT + 16 : FEAT + 16 + SUB, :] = (norm - high).astype(BF16).astype(F32)
            turned_words = y[...].T.astype(BF16)
            for i in range(SUB):
                mask = jnp.where(member == i, 1.0, 0.0).astype(BF16)
                book[q, i * CODES : (i + 1) * CODES, h * 128 : (h + 1) * 128] = turned_words * mask
        return carry

    lax.fori_loop(0, NG // 2, build_book, 0)

    for off in FAR:
        got(at_z(off) * NX + x)
        for d in (1, 3, 2):
            x_copy(at_z(off), d).start()

    def slot_got(d, carry):
        other = lax.rem(p_me + d, NP)
        pltpu.make_async_remote_copy(
            src_ref=slot_out, dst_ref=slots.at[other],
            send_sem=sls_sem.at[0], recv_sem=sl_sem.at[other],
            device_id=(gx, g), device_id_type=MESH,
        ).wait_recv()
        return carry

    lax.fori_loop(1, NP, slot_got, 0)

    def columns(j, carry):
        row = slots[x * NG + j][0:1, :]
        scol[pl.ds(pl.multiple_of(j * ROWS, ROWS), ROWS), :] = jnp.broadcast_to(row, (ROWS, 128)).T
        return carry

    lax.fori_loop(0, NG, columns, 0)
    local = lax.rem(lax.broadcasted_iota(jnp.int32, (128, 128), 0), OWN)

    def places(pp, carry):
        for h in range(2):
            at = slots[2 * pp + h][1:2, :].astype(jnp.int32)
            owner = at // OWN
            zrow[pp, :, h * 128 : (h + 1) * 128] = jnp.broadcast_to(
                jnp.where(owner % NX == x, (owner // NX).astype(F32), -1.0), (8, 128)
            )
            hit = jnp.broadcast_to(at % OWN, (128, 128)) == local
            bt[pp, :, h * 128 : (h + 1) * 128] = jnp.where(hit, 1.0, 0.0).astype(BF16)
        return carry

    lax.fori_loop(0, NP // 2, places, 0)

    lane_all = lax.broadcasted_iota(jnp.int32, (NG * ROWS, 128), 1).astype(F32)
    first = True
    for off in [0] + NEAR[2:] + NEAR[:2] + FAR:
        cz = at_z(off)
        for d in (1, 3, 2):
            got(cz * NX + lax.rem(x + d, NX))
        base = (cz * (NX * OWN)).astype(F32)
        here = scol[...] - base
        pick = jnp.concatenate(
            [jnp.where(here == lane_all + float(128 * h), 1.0, 0.0).astype(BF16) for h in range(2)],
            axis=1,
        )
        rows = cg[pl.ds(cz * NX, NX)].reshape(NX * OWN, FEAT)
        part = jnp.dot(pick, rows, preferred_element_type=F32)
        if first:
            acc[...] = part
        else:
            acc[...] += part
        first = False
    wout[...] = acc[...].astype(BF16).reshape(NG, ROWS, FEAT)

    def pick_copy(d):
        to = lax.rem(g + d, NG)
        return pltpu.make_async_remote_copy(
            src_ref=wout.at[to], dst_ref=win.at[g],
            send_sem=ws_sem.at[d], recv_sem=w_sem.at[g],
            device_id=(gx, to), device_id_type=MESH,
        )

    for d in range(1, NG):
        pick_copy(d).start()
    win[g] = wout[g]
    for d in range(1, NG):
        other = lax.rem(g + d, NG)
        pltpu.make_async_remote_copy(
            src_ref=wout.at[0], dst_ref=win.at[other],
            send_sem=ws_sem.at[0], recv_sem=w_sem.at[other],
            device_id=(gx, g), device_id_type=MESH,
        ).wait_recv()

    turned = vr[...]
    for j in range(NG):
        turned = turned - jnp.dot(
            win[j], rot[j * FEAT : (j + 1) * FEAT, :], preferred_element_type=F32
        )
    tt[...] = turned.T
    for j in range(NG):
        q, h = j // 2, j % 2
        wt[q, h * 128 : h * 128 + FEAT, h * 128 : (h + 1) * 128] = tt[
            j * FEAT : (j + 1) * FEAT, :
        ].astype(BF16)

    def search(i, carry):
        for q in range(NG // 2):
            dist = jnp.dot(
                book[q, pl.ds(pl.multiple_of(i * CODES, CODES), CODES), :], wt[q],
                preferred_element_type=F32,
            )
            low = jnp.min(dist, axis=0, keepdims=True)
            qmin[2 * q, pl.ds(i, 1), :] = low[:, :128]
            qmin[2 * q + 1, pl.ds(i, 1), :] = low[:, 128:]
        return carry

    lax.fori_loop(0, SUB, search, 0)

    qt[...] = jnp.zeros_like(qt)
    for j in range(NG):
        part = tt[j * FEAT : (j + 1) * FEAT, :].reshape(SUB, 8, ROWS)
        err = jnp.sum(part * part, axis=1) + qmin[j, 0:SUB, :]
        qt[j * SUB : (j + 1) * SUB, :] = err
        eout[j] = jnp.concatenate([err, jnp.ones((4, ROWS), F32)], axis=0).astype(BF16)

    def err_copy(d):
        to = lax.rem(p_me + d, NP)
        return pltpu.make_async_remote_copy(
            src_ref=eout.at[to % NG], dst_ref=ein.at[p_me],
            send_sem=es_sem.at[d], recv_sem=e_sem.at[p_me],
            device_id=plane_dev(to), device_id_type=MESH,
        )

    def send_err(d, carry):
        err_copy(d).start()
        return carry

    lax.fori_loop(1, NP, send_err, 0)
    ein[p_me] = eout[g]

    qout[...] = qt[...].T[:, : NG * SUB]
    q_store = pltpu.make_async_copy(qout, q_hbm, out_sem.at[0])
    q_store.start()

    def err_got(d, carry):
        other = lax.rem(p_me + d, NP)
        pltpu.make_async_remote_copy(
            src_ref=eout.at[0], dst_ref=ein.at[other],
            send_sem=es_sem.at[0], recv_sem=e_sem.at[other],
            device_id=(gx, g), device_id_type=MESH,
        ).wait_recv()
        return carry

    lax.fori_loop(1, NP, err_got, 0)

    def sums(pp, total):
        for h in range(2):
            err = ein[2 * pp + h].astype(F32)
            owner = zrow[pp, 0:1, h * 128 : (h + 1) * 128]
            for a in range(NZ):
                lm[a * 16 : (a + 1) * 16, h * 128 : (h + 1) * 128] = jnp.where(
                    owner == float(a), err, 0.0
                ).astype(BF16)
        return total + lax.dot_general(
            lm[...], bt[pp], (((1,), (1,)), ((), ())), preferred_element_type=F32
        )

    total = lax.fori_loop(0, NP // 2, sums, jnp.zeros((NZ * 16, 128), F32))
    lane8 = lax.broadcasted_iota(jnp.int32, (8, 128), 1)
    for a in range(NZ):
        pout[a] = jnp.where(lane8 < OWN, total[a * 16 : a * 16 + 8, :], total[a * 16 + 8 : a * 16 + 16, :])

    def sum_copy(d):
        to = at_z(d)
        return pltpu.make_async_remote_copy(
            src_ref=pout.at[to], dst_ref=pin.at[z],
            send_sem=ps_sem.at[d], recv_sem=p_sem.at[z],
            device_id=(to * NX + x, g), device_id_type=MESH,
        )

    for d in range(1, NZ):
        sum_copy(d).start()
    pin[z] = pout[z]
    for d in range(1, NZ):
        other = at_z(d)
        pltpu.make_async_remote_copy(
            src_ref=pout.at[0], dst_ref=pin.at[other],
            send_sem=ps_sem.at[0], recv_sem=p_sem.at[other],
            device_id=(gx, g), device_id_type=MESH,
        ).wait_recv()
    whole = jnp.sum(pin[...], axis=0)
    count = jnp.broadcast_to(whole[4:5, :], (8, 128))
    count = jnp.where(lane8 < OWN, pltpu.roll(count, OWN, 1), count)
    mean = (whole / jnp.maximum(count, 1.0)).T
    lout[:, 0:8] = mean[0:OWN, :]
    lout[:, 8:SUB] = mean[OWN : 2 * OWN, 0 : SUB - 8]
    l_store = pltpu.make_async_copy(lout, le_hbm, out_sem.at[1])
    l_store.start()

    for one in sent:
        one.wait_send()

    def x_done(bz, carry):
        for d in range(1, NX):
            x_copy(bz, d).wait_send()
        return carry

    lax.fori_loop(0, NZ, x_done, 0)
    for d in range(1, NG):
        book_copy(d).wait_send()
        pick_copy(d).wait_send()

    def plane_done(d, carry):
        slot_copy(d).wait_send()
        err_copy(d).wait_send()
        return carry

    lax.fori_loop(1, NP, plane_done, 0)
    for d in range(1, NZ):
        sum_copy(d).wait_send()
    q_store.wait()
    l_store.wait()


def on_device(vectors, list_ids, old_order, new_order, centroids, rotation, codebook):
    dma = pltpu.SemaphoreType.DMA
    any_spec = pl.BlockSpec(memory_space=pl.ANY)
    return pl.pallas_call(
        kernel,
        out_shape=(
            jax.ShapeDtypeStruct((ROWS, NG * SUB), F32),
            jax.ShapeDtypeStruct((OWN, SUB), F32),
        ),
        in_specs=[any_spec] * 7,
        out_specs=(any_spec, any_spec),
        scratch_shapes=[
            pltpu.VMEM((ROWS, 768), BF16),
            pltpu.VMEM((1, 128), jnp.int32),
            pltpu.VMEM((32, 128), jnp.int32),
            pltpu.VMEM((32, 128), jnp.int32),
            pltpu.VMEM((NZ * NX, OWN, FEAT), BF16),
            pltpu.VMEM((768, 768), BF16),
            pltpu.VMEM((NG, SUB, 8, CODES), BF16),
            pltpu.VMEM((8, 128), F32),
            pltpu.VMEM((NP, 8, 128), F32),
            pltpu.VMEM((NG * ROWS, 128), F32),
            pltpu.VMEM((128, CODES), F32),
            pltpu.VMEM((NG // 2, SUB * CODES, 256), BF16),
            pltpu.VMEM((NG // 2, 256, 256), BF16),
            pltpu.VMEM((NG * ROWS, FEAT), F32),
            pltpu.VMEM((NG, ROWS, FEAT), BF16),
            pltpu.VMEM((NG, ROWS, FEAT), BF16),
            pltpu.VMEM((ROWS, 768), F32),
            pltpu.VMEM((NG, 16, ROWS), F32),
            pltpu.VMEM((768, ROWS), F32),
            pltpu.VMEM((128, ROWS), F32),
            pltpu.VMEM((NG, 16, ROWS), BF16),
            pltpu.VMEM((NP, 16, ROWS), BF16),
            pltpu.VMEM((NP // 2, 8, 256), F32),
            pltpu.VMEM((NP // 2, 128, 256), BF16),
            pltpu.VMEM((NZ * 16, 256), BF16),
            pltpu.VMEM((NZ, 8, 128), F32),
            pltpu.VMEM((NZ, 8, 128), F32),
            pltpu.VMEM((ROWS, NG * SUB), F32),
            pltpu.VMEM((OWN, SUB), F32),
            dma((7,)),
            dma((NZ,)),
            dma((NZ * NX,)),
            dma((NZ * NX,)),
            dma((NG,)),
            dma((NG,)),
            dma((NP,)),
            dma((NP,)),
            dma((NG,)),
            dma((NG,)),
            dma((NP,)),
            dma((NP,)),
            dma((NZ,)),
            dma((NZ,)),
            dma((2,)),
        ],
        compiler_params=pltpu.CompilerParams(
            collective_id=0, has_side_effects=True, vmem_limit_bytes=48 * 1024 * 1024
        ),
    )(
        vectors,
        list_ids.reshape(1, ROWS),
        old_order.reshape(32, 128),
        new_order.reshape(32, 128),
        centroids,
        rotation,
        codebook,
    )


def solution(mesh):
    both = ("gx", "gy")
    in_specs = (P(both, None), P(both), P(), P(), P("gx", "gy"), P(), P("gy", None, None))
    out_specs = (P(both, None), P("gx", "gy"))
    return jax.shard_map(
        on_device, mesh=mesh, in_specs=in_specs, out_specs=out_specs, check_vma=False
    )
```

time: 241 us -> 73.1 us (0.30); the launches traced: 236 us -> 72.7 us
  Pallas kernels: 0 us -> 64.9 us
  starting transfers between devices: 58.3 us -> 0 us
  blocking collectives: 54.6 us -> 0 us
  local copies, waits for them, and re-layouts: 47.4 us -> 7.18 us
  waiting for transfers between devices: 37.3 us -> 0 us
  matrix products: 19.1 us -> 0 us
  other arithmetic: 18.2 us -> 0 us
    pallas_call x0 -> x1, Pallas kernels: none -> 64.9 us  [on_device(): pl.pallas_call(kernel, out_shape=(jax.ShapeDtypeStruct((ROWS, NG * SUB),...]
    all_to_all x5 -> x0, starting transfers between devices: 58.3 us -> none  [the longest x2 21.7 us: copy_for_each(): lax.all_to_all(jnp.broadcast_to(shard[None], (devices, *shard.shape)), ax...]
    all_gather x4 -> x0, blocking collectives: 54.6 us -> none  [the longest x2 39.7 us: gathered_by_axis(): nearer = lax.all_gather(shard, axes[-1], axis=dim, tiled=True)]
    all_to_all x5 -> x0, waiting for transfers between devices: 37.3 us -> none  [the longest x1 20.8 us: on_device(): lax.all_to_all(outgoing.reshape(owners, capacity, feature_width), GX, spl...]
    dot_general x16 -> x0, matrix products: 19.1 us -> none  [the longest x12 15.8 us: one_group(): jnp.einsum('rgd,gdk->rgk', lowered_part, book_part, preferred_element_typ...]
    scatter x3 -> x0, local copies, waits for them, and re-layouts: 18.2 us -> none  [the longest x1 15.5 us: on_device(): slot_of = jnp.zeros((list_total,), jnp.int32).at[new_order].set(jnp.arang...]
    reduce_min x12 -> x0, other arithmetic: 14.3 us -> none  [one_group(): return jnp.min(distance, axis=2)]
    add x12 -> x0, local copies, waits for them, and re-layouts: 8.45 us -> none  [one_group(): square_part[:, :, None] - 2.0 * inner_terms + norm_part[None, :, :]]
  transfers between devices with their start and end apart: 5 -> 0, of which waited for: 3 -> 0; matrix products, arithmetic and copies ran while one was open for 7% -> 0% of each run, Pallas kernels for 0% -> 0%
where the time goes in v1:
time: 73.1 us; the launch traced here: 72.7 us
  Pallas kernels  64.9 us (89%)
  local copies, waits for them, and re-layouts  7.18 us (10%)
    pallas_call x1, Pallas kernels, on_device(): pl.pallas_call(kernel, out_shape=(jax.ShapeDtypeStruct((ROWS, NG * SUB),...  64.9 us
    unnamed x14, local copies, waits for them, and re-layouts  5.79 us

profile of v1, /device:TPU:1, one launch (start us, length us, event | category | flops | bytes accessed | tf_op | source)
XLA Modules:
  0.0 72.7 jit_solution(6064328636720497223)
XLA Ops:
  0.6 0.0 copy-start
  0.6 1.3 %copy-done = bf16[768,768]{1,0:T(8,128)(2,1)S(1)} copy-done((bf16[768,768]{1,0:T(8,128)(2,1)S(1)}, bf16[768,768]{1,0:T(8,128)(2,1)}, u32[]{:S(2)}) %copy-start) | copy-done | bytes 1179672
  1.9 0.0 copy-start.1
  1.9 0.9 %copy-done.1 = bf16[128,768]{1,0:T(8,128)(2,1)S(1)} copy-done((bf16[128,768]{1,0:T(8,128)(2,1)S(1)}, bf16[128,768]{1,0:T(8,128)(2,1)}, u32[]{:S(2)}) %copy-start.1) | copy-done | bytes 196632
  2.8 0.0 copy-start.2
  2.8 0.8 %copy-done.2 = bf16[12,8,256]{2,1,0:T(8,128)(2,1)S(1)} copy-done((bf16[12,8,256]{2,1,0:T(8,128)(2,1)S(1)}, bf16[12,8,256]{2,1,0:T(8,128)(2,1)}, u32[]{:S(2)}) %copy-start.2) | copy-done | bytes 49176
  3.6 0.0 copy-start.3
  3.6 0.7 copy-done.3
  4.3 0.0 copy-start.4
  4.3 0.7 copy-done.4
  5.1 0.0 copy-start.5
  5.1 0.7 copy-done.5
  5.8 0.0 copy-start.6
  5.8 0.7 copy-done.6
  6.4 64.9 %shard_map.86 = (f32[128,96]{1,0:T(8,128)S(1)}, f32[64,12]{1,0:T(8,128)S(1)}) custom-call(bf16[128,768]{1,0:T(8,128)(2,1)S(1)} %copy-done.1, s32[1,128]{1,0:T(1,128)S(1)} %bitcast.5, s32[32,128]{1,0:T(8,128)S(1)} %bitcast.3, s32[32,128]{1,0:T(8,128)S(1)} %bitcast.4, bf16[64,96]{1,0:T(8,128)(2,1)S(1)} %copy-done.5, bf16[768,768]{1,0:T(8,128)(2,1)S(1)} %copy-done, ...), custom_call_target="tpu_custom_call" | custom-call | tf_op jit(solution)/shard_map/pallas_call | solution.py:409
  71.4 0.7 copy.9
  72.1 0.7 copy.10
Async XLA Ops:
  0.6 1.3 %copy-start = (bf16[768,768]{1,0:T(8,128)(2,1)S(1)}, bf16[768,768]{1,0:T(8,128)(2,1)}, u32[]{:S(2)}) copy-start(bf16[768,768]{1,0:T(8,128)(2,1)} %r_hbm.1) | copy-start | bytes 3538948
  1.9 0.9 %copy-start.1 = (bf16[128,768]{1,0:T(8,128)(2,1)S(1)}, bf16[128,768]{1,0:T(8,128)(2,1)}, u32[]{:S(2)}) copy-start(bf16[128,768]{1,0:T(8,128)(2,1)} %v_hbm.1) | copy-start | bytes 589828
  2.8 0.8 %copy-start.2 = (bf16[12,8,256]{2,1,0:T(8,128)(2,1)S(1)}, bf16[12,8,256]{2,1,0:T(8,128)(2,1)}, u32[]{:S(2)}) copy-start(bf16[12,8,256]{2,1,0:T(8,128)(2,1)} %cb_hbm.1) | copy-start | bytes 147460
  3.6 0.7 copy-start.3
  4.3 0.7 copy-start.4
  5.1 0.7 copy-start.5
  5.8 0.7 copy-start.6

commit v2 on v1

--- a/solution.py
+++ b/solution.py
@@ -16,6 +16,8 @@
 SUB = 12
 ROWS = 128
 CODES = 256
+CHUNK = 256
+WIDE = 6
 HOP = 4
 NEAR = [4, -4, 1, -1, 2, -2, 3, -3]
 FAR = [5, -5, 6, -6, 7, -7, 8]
@@ -25,8 +27,8 @@
     v_hbm, ids_hbm, old_hbm, new_hbm, c_hbm, r_hbm, cb_hbm,
     q_hbm, le_hbm,
     v, ids, old, new, cg, rot, cb,
-    slot_out, slots, scol, y, book, wt, acc, wout, win, vr,
-    qmin, tt, qt, eout, ein, zrow, bt, lm, pout, pin, qout, lout,
+    slot_out, slots, high, low_hot, y, book, wt, acc, wout, win, vr,
+    qmin, tt, qt, eout, ein, zrow, bt, lm, pout, pin, lout,
     in_sem, zs_sem, xs_sem, ag_sem, cbs_sem, cb_sem, sls_sem, sl_sem,
     ws_sem, w_sem, es_sem, e_sem, ps_sem, p_sem, out_sem,
 ):
@@ -77,7 +79,6 @@
             total = total + jnp.where(id_col == entry, lane_f + float(128 * k), 0.0)
         slot_out[row : row + 1, :] = jnp.sum(total.T, axis=0, keepdims=True)
 
-    slot_out[...] = jnp.zeros((8, 128), F32)
     find(old, 0)
     find(new, 1)
 
@@ -143,10 +144,13 @@
     loads[6].wait()
     vr[...] = jnp.dot(v[...], rot[...], preferred_element_type=F32)
 
-    for off in NEAR[2:]:
-        got(at_z(off) * NX + x)
+    def spread(off):
         for d in (1, 3, 2):
             x_copy(at_z(off), d).start()
+
+    for off in NEAR[2:6]:
+        got(at_z(off) * NX + x)
+        spread(off)
     k = len(NEAR)
     for off in NEAR[:2]:
         got(at_z(off) * NX + x)
@@ -155,9 +159,10 @@
             sent.append(z_copy(at_z(off), step * far, k))
             sent[-1].start()
             k += 1
-    for off in NEAR[:2]:
-        for d in (1, 3, 2):
-            x_copy(at_z(off), d).start()
+    for off in NEAR[6:] + NEAR[:2]:
+        if abs(off) < HOP:
+            got(at_z(off) * NX + x)
+        spread(off)
 
     y[...] = jnp.zeros_like(y)
     wt[...] = jnp.zeros_like(wt)
@@ -195,11 +200,6 @@
 
     lax.fori_loop(0, NG // 2, build_book, 0)
 
-    for off in FAR:
-        got(at_z(off) * NX + x)
-        for d in (1, 3, 2):
-            x_copy(at_z(off), d).start()
-
     def slot_got(d, carry):
         other = lax.rem(p_me + d, NP)
         pltpu.make_async_remote_copy(
@@ -212,8 +212,14 @@
     lax.fori_loop(1, NP, slot_got, 0)
 
     def columns(j, carry):
-        row = slots[x * NG + j][0:1, :]
-        scol[pl.ds(pl.multiple_of(j * ROWS, ROWS), ROWS), :] = jnp.broadcast_to(row, (ROWS, 128)).T
+        row = slots[x * NG + j][0:1, :].astype(jnp.int32)
+        at = pl.ds(pl.multiple_of(j * ROWS, ROWS), ROWS)
+        high[at, :] = jnp.broadcast_to((row // CHUNK).astype(F32), (ROWS, 128)).T
+        rest = jnp.broadcast_to((row % CHUNK).astype(F32), (ROWS, 128)).T
+        for h in range(2):
+            low_hot[at, h * 128 : (h + 1) * 128] = jnp.where(
+                rest == lane_f + float(128 * h), 1.0, 0.0
+            ).astype(BF16)
         return carry
 
     lax.fori_loop(0, NG, columns, 0)
@@ -230,28 +236,36 @@
             bt[pp, :, h * 128 : (h + 1) * 128] = jnp.where(hit, 1.0, 0.0).astype(BF16)
         return carry
 
+    for off in FAR:
+        got(at_z(off) * NX + x)
+        spread(off)
+
     lax.fori_loop(0, NP // 2, places, 0)
 
-    lane_all = lax.broadcasted_iota(jnp.int32, (NG * ROWS, 128), 1).astype(F32)
-    first = True
-    for off in [0] + NEAR[2:] + NEAR[:2] + FAR:
-        cz = at_z(off)
-        for d in (1, 3, 2):
-            got(cz * NX + lax.rem(x + d, NX))
-        base = (cz * (NX * OWN)).astype(F32)
-        here = scol[...] - base
-        pick = jnp.concatenate(
-            [jnp.where(here == lane_all + float(128 * h), 1.0, 0.0).astype(BF16) for h in range(2)],
-            axis=1,
-        )
-        rows = cg[pl.ds(cz * NX, NX)].reshape(NX * OWN, FEAT)
-        part = jnp.dot(pick, rows, preferred_element_type=F32)
-        if first:
-            acc[...] = part
-        else:
-            acc[...] += part
-        first = False
-    wout[...] = acc[...].astype(BF16).reshape(NG, ROWS, FEAT)
+    acc[...] = jnp.zeros_like(acc)
+    blank = jnp.zeros((CHUNK, 128 - FEAT), BF16)
+
+    def pick(offs):
+        sides = []
+        for off in offs:
+            cz = at_z(off)
+            for d in (1, 3, 2):
+                got(cz * NX + lax.rem(x + d, NX))
+            rows = cg[pl.ds(cz * NX, NX)].reshape(CHUNK, FEAT)
+            sides.append(jnp.concatenate([rows, blank], axis=1))
+        both = jnp.concatenate(sides, axis=1)
+        za, zb = (at_z(off).astype(F32) for off in offs)
+        part = jnp.dot(low_hot[...], both, preferred_element_type=F32)
+        acc[...] = jnp.where(
+            high[...] == za, part[:, :128], jnp.where(high[...] == zb, part[:, 128:], acc[...])
+        )
+
+    order = [0, 1, -1, 2, -2, 3, -3, 4, -4] + FAR
+    for k in range(0, NZ, 2):
+        if k == 8:
+            pass
+        pick(order[k : k + 2])
+    wout[...] = acc[:, :FEAT].astype(BF16).reshape(NG, ROWS, FEAT)
 
     def pick_copy(d):
         to = lax.rem(g + d, NG)
@@ -284,20 +298,15 @@
             j * FEAT : (j + 1) * FEAT, :
         ].astype(BF16)
 
-    def search(i, carry):
-        for q in range(NG // 2):
+    for q in range(NG // 2):
+        for i in range(0, SUB, WIDE):
             dist = jnp.dot(
-                book[q, pl.ds(pl.multiple_of(i * CODES, CODES), CODES), :], wt[q],
-                preferred_element_type=F32,
+                book[q, i * CODES : (i + WIDE) * CODES, :], wt[q], preferred_element_type=F32
             )
-            low = jnp.min(dist, axis=0, keepdims=True)
-            qmin[2 * q, pl.ds(i, 1), :] = low[:, :128]
-            qmin[2 * q + 1, pl.ds(i, 1), :] = low[:, 128:]
-        return carry
-
-    lax.fori_loop(0, SUB, search, 0)
-
-    qt[...] = jnp.zeros_like(qt)
+            low = jnp.min(dist.reshape(WIDE, CODES, 256), axis=1)
+            qmin[2 * q, i : i + WIDE, :] = low[:, :128]
+            qmin[2 * q + 1, i : i + WIDE, :] = low[:, 128:]
+
     for j in range(NG):
         part = tt[j * FEAT : (j + 1) * FEAT, :].reshape(SUB, 8, ROWS)
         err = jnp.sum(part * part, axis=1) + qmin[j, 0:SUB, :]
@@ -319,8 +328,7 @@
     lax.fori_loop(1, NP, send_err, 0)
     ein[p_me] = eout[g]
 
-    qout[...] = qt[...].T[:, : NG * SUB]
-    q_store = pltpu.make_async_copy(qout, q_hbm, out_sem.at[0])
+    q_store = pltpu.make_async_copy(qt, q_hbm, out_sem.at[0])
     q_store.start()
 
     def err_got(d, carry):
@@ -339,14 +347,16 @@
             err = ein[2 * pp + h].astype(F32)
             owner = zrow[pp, 0:1, h * 128 : (h + 1) * 128]
             for a in range(NZ):
-                lm[a * 16 : (a + 1) * 16, h * 128 : (h + 1) * 128] = jnp.where(
+                lm[pp, a * 16 : (a + 1) * 16, h * 128 : (h + 1) * 128] = jnp.where(
                     owner == float(a), err, 0.0
                 ).astype(BF16)
         return total + lax.dot_general(
-            lm[...], bt[pp], (((1,), (1,)), ((), ())), preferred_element_type=F32
-        )
-
-    total = lax.fori_loop(0, NP // 2, sums, jnp.zeros((NZ * 16, 128), F32))
+            lm[pp], bt[pp], (((1,), (1,)), ((), ())), preferred_element_type=F32
+        )
+
+    total = jnp.zeros((NZ * 16, 128), F32)
+    for pp in range(NP // 2):
+        total = sums(pp, total)
     lane8 = lax.broadcasted_iota(jnp.int32, (8, 128), 1)
     for a in range(NZ):
         pout[a] = jnp.where(lane8 < OWN, total[a * 16 : a * 16 + 8, :], total[a * 16 + 8 : a * 16 + 16, :])
@@ -372,9 +382,9 @@
     whole = jnp.sum(pin[...], axis=0)
     count = jnp.broadcast_to(whole[4:5, :], (8, 128))
     count = jnp.where(lane8 < OWN, pltpu.roll(count, OWN, 1), count)
-    mean = (whole / jnp.maximum(count, 1.0)).T
-    lout[:, 0:8] = mean[0:OWN, :]
-    lout[:, 8:SUB] = mean[OWN : 2 * OWN, 0 : SUB - 8]
+    mean = whole / jnp.maximum(count, 1.0)
+    lout[0:8, :] = mean[:, :OWN]
+    lout[8:SUB, :] = pltpu.roll(mean, OWN, 1)[: SUB - 8, :OWN]
     l_store = pltpu.make_async_copy(lout, le_hbm, out_sem.at[1])
     l_store.start()
 
@@ -405,12 +415,12 @@
 
 def on_device(vectors, list_ids, old_order, new_order, centroids, rotation, codebook):
     dma = pltpu.SemaphoreType.DMA
-    any_spec = pl.BlockSpec(memory_space=pl.ANY)
-    return pl.pallas_call(
+    any_spec = pl.BlockSpec(memory_space=pltpu.HBM)
+    errors, means = pl.pallas_call(
         kernel,
         out_shape=(
-            jax.ShapeDtypeStruct((ROWS, NG * SUB), F32),
-            jax.ShapeDtypeStruct((OWN, SUB), F32),
+            jax.ShapeDtypeStruct((NG * SUB, ROWS), F32),
+            jax.ShapeDtypeStruct((SUB, OWN), F32),
         ),
         in_specs=[any_spec] * 7,
         out_specs=(any_spec, any_spec),
@@ -422,28 +432,28 @@
             pltpu.VMEM((NZ * NX, OWN, FEAT), BF16),
             pltpu.VMEM((768, 768), BF16),
             pltpu.VMEM((NG, SUB, 8, CODES), BF16),
-            pltpu.VMEM((8, 128), F32),
-            pltpu.VMEM((NP, 8, 128), F32),
+            pltpu.VMEM((2, 128), F32),
+            pltpu.VMEM((NP, 2, 128), F32),
             pltpu.VMEM((NG * ROWS, 128), F32),
+            pltpu.VMEM((NG * ROWS, 256), BF16),
             pltpu.VMEM((128, CODES), F32),
             pltpu.VMEM((NG // 2, SUB * CODES, 256), BF16),
             pltpu.VMEM((NG // 2, 256, 256), BF16),
-            pltpu.VMEM((NG * ROWS, FEAT), F32),
+            pltpu.VMEM((NG * ROWS, 128), F32),
             pltpu.VMEM((NG, ROWS, FEAT), BF16),
             pltpu.VMEM((NG, ROWS, FEAT), BF16),
             pltpu.VMEM((ROWS, 768), F32),
             pltpu.VMEM((NG, 16, ROWS), F32),
             pltpu.VMEM((768, ROWS), F32),
-            pltpu.VMEM((128, ROWS), F32),
+            pltpu.VMEM((NG * SUB, ROWS), F32),
             pltpu.VMEM((NG, 16, ROWS), BF16),
             pltpu.VMEM((NP, 16, ROWS), BF16),
             pltpu.VMEM((NP // 2, 8, 256), F32),
             pltpu.VMEM((NP // 2, 128, 256), BF16),
-            pltpu.VMEM((NZ * 16, 256), BF16),
+            pltpu.VMEM((NP // 2, NZ * 16, 256), BF16),
             pltpu.VMEM((NZ, 8, 128), F32),
             pltpu.VMEM((NZ, 8, 128), F32),
-            pltpu.VMEM((ROWS, NG * SUB), F32),
-            pltpu.VMEM((OWN, SUB), F32),
+            pltpu.VMEM((SUB, OWN), F32),
             dma((7,)),
             dma((NZ,)),
             dma((NZ * NX,)),
@@ -461,7 +471,7 @@
             dma((2,)),
         ],
         compiler_params=pltpu.CompilerParams(
-            collective_id=0, has_side_effects=True, vmem_limit_bytes=48 * 1024 * 1024
+            collective_id=0, has_side_effects=True, vmem_limit_bytes=67043328
         ),
     )(
         vectors,
@@ -472,6 +482,7 @@
         rotation,
         codebook,
     )
+    return errors.T, means.T
 
 
 def solution(mesh):

time: 73.1 us -> 63 us (0.86); the launches traced: 72.7 us -> 61.8 us
  Pallas kernels: 64.9 us -> 58.4 us
  local copies, waits for them, and re-layouts: 7.18 us -> 2.72 us
    pallas_call x1, Pallas kernels: 64.9 us -> 58.4 us  [on_device(): pl.pallas_call(kernel, out_shape=(jax.ShapeDtypeStruct((NG * SUB, ROWS),...]
    unnamed x14 -> x2, local copies, waits for them, and re-layouts: 5.79 us -> 2.72 us
    pallas_call x2 -> x0, local copies, waits for them, and re-layouts: 1.39 us -> none  [on_device(): pl.pallas_call(kernel, out_shape=(jax.ShapeDtypeStruct((ROWS, NG * SUB),...]
where the time goes in v2:
time: 63 us; the launch traced here: 61.8 us
  Pallas kernels  58.4 us (93%)
  local copies, waits for them, and re-layouts  2.72 us (4%)
  between operations  0.64 us (1%)
    pallas_call x1, Pallas kernels, on_device(): pl.pallas_call(kernel, out_shape=(jax.ShapeDtypeStruct((NG * SUB, ROWS),...  58.4 us
    unnamed x2, local copies, waits for them, and re-layouts  2.72 us

profile of v2, /device:TPU:1, one launch (start us, length us, event | category | flops | bytes accessed | tf_op | source)
XLA Modules:
  0.0 61.8 jit_solution(7112584549943713151)
XLA Ops:
  0.6 58.4 %shard_map.86 = (f32[96,128]{1,0:T(8,128)}, f32[12,64]{1,0:T(8,128)}) custom-call(bf16[128,768]{1,0:T(8,128)(2,1)} %v_hbm.1, s32[1,128]{1,0:T(1,128)} %bitcast.9, s32[32,128]{1,0:T(8,128)} %bitcast.6, s32[32,128]{1,0:T(8,128)} %bitcast.7, bf16[64,96]{1,0:T(8,128)(2,1)} %c_hbm.1, bf16[768,768]{1,0:T(8,128)(2,1)} %r_hbm.1, bf16[12,8,256]{2,1,0:T(8,128)(2,1)} %cb_hbm.1), custom_call_target="tpu_custom_call" | custom-call | tf_op jit(solution)/shard_map/pallas_call | solution.py:419
  59.0 1.4 %copy.11 = f32[128,96]{0,1:T(8,128)} copy(f32[128,96]{0,1:T(8,128)} %bitcast.5) | data formatting | bytes 98304
  60.5 1.3 %copy.12 = f32[64,12]{0,1:T(8,128)} copy(f32[64,12]{0,1:T(8,128)} %bitcast.8) | data formatting | bytes 6144

commit v3 on v2

--- a/solution.py
+++ b/solution.py
@@ -1,3 +1,5 @@
+import itertools
+
 import jax
 import jax.numpy as jnp
 from jax import lax
@@ -17,6 +19,7 @@
 ROWS = 128
 CODES = 256
 CHUNK = 256
+PACKED = OWN * FEAT // 128
 WIDE = 6
 HOP = 4
 NEAR = [4, -4, 1, -1, 2, -2, 3, -3]
@@ -26,7 +29,7 @@
 def kernel(
     v_hbm, ids_hbm, old_hbm, new_hbm, c_hbm, r_hbm, cb_hbm,
     q_hbm, le_hbm,
-    v, ids, old, new, cg, rot, cb,
+    v, ids, old, new, block_in, cg, rot, cb,
     slot_out, slots, high, low_hot, y, book, wt, acc, wout, win, vr,
     qmin, tt, qt, eout, ein, zrow, bt, lm, pout, pin, lout,
     in_sem, zs_sem, xs_sem, ag_sem, cbs_sem, cb_sem, sls_sem, sl_sem,
@@ -39,11 +42,13 @@
     def at_z(off):
         return lax.rem(z + (off + NZ), NZ)
 
-    def plane_dev(p):
-        return (z * NX + p // NG, p % NG)
+    x_to = [lax.rem(x + d, NX) for d in range(NX)]
+    g_to = [lax.rem(g + d, NG) for d in range(NG)]
+    gx_to = [z * NX + one for one in x_to]
+    plane = [(dx, dg) for dx in (2, 1, 3, 0) for dg in (4, 5, 2, 3, 6, 7, 1, 0) if dx or dg]
 
     loads = [
-        pltpu.make_async_copy(c_hbm, cg.at[gx], in_sem.at[0]),
+        pltpu.make_async_copy(c_hbm, block_in, in_sem.at[0]),
         pltpu.make_async_copy(ids_hbm, ids, in_sem.at[1]),
         pltpu.make_async_copy(old_hbm, old, in_sem.at[2]),
         pltpu.make_async_copy(new_hbm, new, in_sem.at[3]),
@@ -58,13 +63,46 @@
     for off in NEAR:
         pl.semaphore_signal(barrier, inc=1, device_id=(at_z(off) * NX + x, g), device_id_type=MESH)
 
-    def greet(d, carry):
-        pl.semaphore_signal(
-            barrier, inc=1, device_id=plane_dev(lax.rem(p_me + d, NP)), device_id_type=MESH
-        )
-        return carry
-
-    lax.fori_loop(1, NP, greet, 0)
+    for dx, dg in plane:
+        pl.semaphore_signal(barrier, inc=1, device_id=(gx_to[dx], g_to[dg]), device_id_type=MESH)
+
+    loads[0].wait()
+    for k in range(3):
+        tail = block_in[48:64, 32 * k : 32 * (k + 1)]
+        cg[gx, 16 * k : 16 * (k + 1), :] = jnp.concatenate(
+            [block_in[16 * k : 16 * (k + 1), :], tail], axis=1
+        )
+    pl.semaphore_wait(barrier, len(NEAR) + NP - 1)
+
+    def z_copy(block_z, to_off, k):
+        block = block_z * NX + x
+        return pltpu.make_async_remote_copy(
+            src_ref=cg.at[block], dst_ref=cg.at[block],
+            send_sem=zs_sem.at[k], recv_sem=ag_sem.at[block],
+            device_id=(at_z(to_off) * NX + x, g), device_id_type=MESH,
+        )
+
+    def x_copy(block_z, d):
+        block = block_z * NX + x
+        return pltpu.make_async_remote_copy(
+            src_ref=cg.at[block], dst_ref=cg.at[block],
+            send_sem=xs_sem.at[block_z * NX + d], recv_sem=ag_sem.at[block],
+            device_id=(z * NX + lax.rem(x + d, NX), g), device_id_type=MESH,
+        )
+
+    def got(block):
+        pltpu.make_async_remote_copy(
+            src_ref=cg.at[block], dst_ref=cg.at[block],
+            send_sem=zs_sem.at[0], recv_sem=ag_sem.at[block],
+            device_id=(gx, g), device_id_type=MESH,
+        ).wait_recv()
+
+    sent = []
+    for k, off in enumerate(NEAR):
+        sent.append(z_copy(z, off, k))
+        sent[-1].start()
+    for d in (1, 3, 2):
+        x_copy(z, d).start()
 
     for k in (1, 2, 3):
         loads[k].wait()
@@ -82,52 +120,15 @@
     find(old, 0)
     find(new, 1)
 
-    loads[0].wait()
-    loads[4].wait()
-    pl.semaphore_wait(barrier, len(NEAR) + NP - 1)
-
-    def z_copy(block_z, to_off, k):
-        block = block_z * NX + x
-        return pltpu.make_async_remote_copy(
-            src_ref=cg.at[block], dst_ref=cg.at[block],
-            send_sem=zs_sem.at[k], recv_sem=ag_sem.at[block],
-            device_id=(at_z(to_off) * NX + x, g), device_id_type=MESH,
-        )
-
-    def x_copy(block_z, d):
-        block = block_z * NX + x
-        return pltpu.make_async_remote_copy(
-            src_ref=cg.at[block], dst_ref=cg.at[block],
-            send_sem=xs_sem.at[block_z * NX + d], recv_sem=ag_sem.at[block],
-            device_id=(z * NX + lax.rem(x + d, NX), g), device_id_type=MESH,
-        )
-
-    def got(block):
-        pltpu.make_async_remote_copy(
-            src_ref=cg.at[block], dst_ref=cg.at[block],
-            send_sem=zs_sem.at[0], recv_sem=ag_sem.at[block],
-            device_id=(gx, g), device_id_type=MESH,
-        ).wait_recv()
-
-    sent = []
-    for k, off in enumerate(NEAR):
-        sent.append(z_copy(z, off, k))
-        sent[-1].start()
-    for d in (1, 3, 2):
-        x_copy(z, d).start()
-
-    def slot_copy(d):
+    def slot_copy(dx, dg):
         return pltpu.make_async_remote_copy(
             src_ref=slot_out, dst_ref=slots.at[p_me],
-            send_sem=sls_sem.at[d], recv_sem=sl_sem.at[p_me],
-            device_id=plane_dev(lax.rem(p_me + d, NP)), device_id_type=MESH,
-        )
-
-    def send_slots(d, carry):
-        slot_copy(d).start()
-        return carry
-
-    lax.fori_loop(1, NP, send_slots, 0)
+            send_sem=sls_sem.at[dx * NG + dg], recv_sem=sl_sem.at[p_me],
+            device_id=(gx_to[dx], g_to[dg]), device_id_type=MESH,
+        )
+
+    for dx, dg in plane:
+        slot_copy(dx, dg).start()
     slots[p_me] = slot_out[...]
 
     def book_copy(d):
@@ -137,6 +138,7 @@
             device_id=(gx, lax.rem(g + d, NG)), device_id_type=MESH,
         )
 
+    loads[4].wait()
     for d in range(1, NG):
         book_copy(d).start()
 
@@ -181,9 +183,6 @@
     lane_row = lax.broadcasted_iota(jnp.int32, (1, 128), 1)
     member = jnp.where(lane_row < FEAT, lane_row // 8, lax.rem(lane_row - FEAT, 16))
 
-    for d in range(1, NG):
-        book_got(d)
-
     def build_book(q, carry):
         for h in range(2):
             words = cb[2 * q + h].astype(F32)
@@ -198,7 +197,6 @@
                 book[q, i * CODES : (i + 1) * CODES, h * 128 : (h + 1) * 128] = turned_words * mask
         return carry
 
-    lax.fori_loop(0, NG // 2, build_book, 0)
 
     def slot_got(d, carry):
         other = lax.rem(p_me + d, NP)
@@ -215,10 +213,13 @@
         row = slots[x * NG + j][0:1, :].astype(jnp.int32)
         at = pl.ds(pl.multiple_of(j * ROWS, ROWS), ROWS)
         high[at, :] = jnp.broadcast_to((row // CHUNK).astype(F32), (ROWS, 128)).T
-        rest = jnp.broadcast_to((row % CHUNK).astype(F32), (ROWS, 128)).T
+        inner = row % CHUNK
+        block, spot = inner // OWN, inner % OWN
+        place = jnp.where(spot < 48, block * 48 + spot, 144 + block * 16 + spot)
+        rest = jnp.broadcast_to(place.astype(F32), (ROWS, 128)).T
         for h in range(2):
             low_hot[at, h * 128 : (h + 1) * 128] = jnp.where(
-                rest == lane_f + float(128 * h), 1.0, 0.0
+                rest == lane_f + float(128 * h), -1.0, 0.0
             ).astype(BF16)
         return carry
 
@@ -236,67 +237,101 @@
             bt[pp, :, h * 128 : (h + 1) * 128] = jnp.where(hit, 1.0, 0.0).astype(BF16)
         return carry
 
-    for off in FAR:
-        got(at_z(off) * NX + x)
-        spread(off)
-
-    lax.fori_loop(0, NP // 2, places, 0)
-
     acc[...] = jnp.zeros_like(acc)
-    blank = jnp.zeros((CHUNK, 128 - FEAT), BF16)
-
-    def pick(offs):
+    blank = jnp.zeros((16, 128 - FEAT), BF16)
+
+    def operand(offs):
         sides = []
         for off in offs:
             cz = at_z(off)
             for d in (1, 3, 2):
                 got(cz * NX + lax.rem(x + d, NX))
-            rows = cg[pl.ds(cz * NX, NX)].reshape(CHUNK, FEAT)
-            sides.append(jnp.concatenate([rows, blank], axis=1))
-        both = jnp.concatenate(sides, axis=1)
+            blocks = [cg[cz * NX + b] for b in range(NX)]
+            tails = [
+                jnp.concatenate(
+                    [one[16 * k : 16 * (k + 1), FEAT:] for k in range(3)] + [blank], axis=1
+                )
+                for one in blocks
+            ]
+            sides.append(jnp.concatenate(blocks + tails, axis=0))
+        return jnp.concatenate(sides, axis=1)
+
+    def choose(part, offs, hi, before):
         za, zb = (at_z(off).astype(F32) for off in offs)
-        part = jnp.dot(low_hot[...], both, preferred_element_type=F32)
-        acc[...] = jnp.where(
-            high[...] == za, part[:, :128], jnp.where(high[...] == zb, part[:, 128:], acc[...])
-        )
+        return jnp.where(hi == za, part[:, :128], jnp.where(hi == zb, part[:, 128:], before))
+
+    def pick(offs):
+        part = jnp.dot(low_hot[...], operand(offs), preferred_element_type=F32)
+        acc[...] = choose(part, offs, high[...], acc[...])
 
     order = [0, 1, -1, 2, -2, 3, -3, 4, -4] + FAR
-    for k in range(0, NZ, 2):
-        if k == 8:
-            pass
+    pick(order[0:2])
+    pick(order[2:4])
+    for off in FAR[:4]:
+        got(at_z(off) * NX + x)
+        spread(off)
+    pick(order[4:6])
+    for off in FAR[4:]:
+        got(at_z(off) * NX + x)
+        spread(off)
+    pick(order[6:8])
+    for d in range(1, NG):
+        book_got(d)
+    lax.fori_loop(0, NG // 4, build_book, 0)
+    for k in range(NZ // 2, NZ - 2, 2):
         pick(order[k : k + 2])
-    wout[...] = acc[:, :FEAT].astype(BF16).reshape(NG, ROWS, FEAT)
-
-    def pick_copy(d):
-        to = lax.rem(g + d, NG)
+
+    def pick_copy(to, k):
         return pltpu.make_async_remote_copy(
             src_ref=wout.at[to], dst_ref=win.at[g],
-            send_sem=ws_sem.at[d], recv_sem=w_sem.at[g],
+            send_sem=ws_sem.at[k], recv_sem=w_sem.at[g],
             device_id=(gx, to), device_id_type=MESH,
         )
 
-    for d in range(1, NG):
-        pick_copy(d).start()
+    last = order[NZ - 2 :]
+    final = operand(last)
+    y_me, core = g // 2, g % 2
+    for dy in (2, 1, 3, 0):
+        chip = lax.rem(y_me + dy, NG // 2)
+        at = pl.ds(pl.multiple_of(chip * 2 * ROWS, 2 * ROWS), 2 * ROWS)
+        part = jnp.dot(low_hot[at, :], final, preferred_element_type=F32)
+        rows = choose(part, last, high[at, :], acc[at, :]).astype(BF16)
+        for c in range(2):
+            mine = rows[c * ROWS : (c + 1) * ROWS]
+            for k in range(3):
+                wout[2 * chip + c, 32 * k : 32 * (k + 1), :] = jnp.concatenate(
+                    [mine[32 * k : 32 * (k + 1), :FEAT], mine[FEAT:, 32 * k : 32 * (k + 1)]], axis=1
+                )
+        if dy:
+            for c in range(2):
+                pick_copy(2 * chip + c, 2 * dy + c).start()
+        else:
+            pick_copy(2 * chip + 1 - core, 0).start()
     win[g] = wout[g]
-    for d in range(1, NG):
-        other = lax.rem(g + d, NG)
-        pltpu.make_async_remote_copy(
-            src_ref=wout.at[0], dst_ref=win.at[other],
-            send_sem=ws_sem.at[0], recv_sem=w_sem.at[other],
-            device_id=(gx, g), device_id_type=MESH,
-        ).wait_recv()
-
-    turned = vr[...]
-    for j in range(NG):
-        turned = turned - jnp.dot(
-            win[j], rot[j * FEAT : (j + 1) * FEAT, :], preferred_element_type=F32
-        )
-    tt[...] = turned.T
+
+    lax.fori_loop(NG // 4, NG // 2, build_book, 0)
+    come = [g, 2 * y_me + 1 - core]
+    for dy in (1, 3, 2):
+        come += [2 * lax.rem(y_me + dy, NG // 2) + c for c in range(2)]
+    for k, other in enumerate(come):
+        if k:
+            pltpu.make_async_remote_copy(
+                src_ref=wout.at[0], dst_ref=win.at[other],
+                send_sem=ws_sem.at[0], recv_sem=w_sem.at[other],
+                device_id=(gx, g), device_id_type=MESH,
+            ).wait_recv()
+        packed = win[other]
+        tail = jnp.concatenate([packed[32 * k : 32 * (k + 1), FEAT:] for k in range(3)], axis=1)
+        rows = jnp.concatenate([packed[:, :FEAT], tail], axis=0)
+        vr[...] += jnp.dot(
+            rows, rot[pl.ds(pl.multiple_of(other * FEAT, 32), FEAT), :], preferred_element_type=F32
+        )
+    tt[...] = vr[...].T
     for j in range(NG):
         q, h = j // 2, j % 2
-        wt[q, h * 128 : h * 128 + FEAT, h * 128 : (h + 1) * 128] = tt[
-            j * FEAT : (j + 1) * FEAT, :
-        ].astype(BF16)
+        part = tt[j * FEAT : (j + 1) * FEAT, :]
+        wt[q, h * 128 : h * 128 + FEAT, h * 128 : (h + 1) * 128] = part.astype(BF16)
+        qt[j * SUB : (j + 1) * SUB, :] = jnp.sum((part * part).reshape(SUB, 8, ROWS), axis=1)
 
     for q in range(NG // 2):
         for i in range(0, SUB, WIDE):
@@ -308,41 +343,40 @@
             qmin[2 * q + 1, i : i + WIDE, :] = low[:, 128:]
 
     for j in range(NG):
-        part = tt[j * FEAT : (j + 1) * FEAT, :].reshape(SUB, 8, ROWS)
-        err = jnp.sum(part * part, axis=1) + qmin[j, 0:SUB, :]
+        err = qt[j * SUB : (j + 1) * SUB, :] + qmin[j, 0:SUB, :]
         qt[j * SUB : (j + 1) * SUB, :] = err
         eout[j] = jnp.concatenate([err, jnp.ones((4, ROWS), F32)], axis=0).astype(BF16)
 
-    def err_copy(d):
-        to = lax.rem(p_me + d, NP)
-        return pltpu.make_async_remote_copy(
-            src_ref=eout.at[to % NG], dst_ref=ein.at[p_me],
-            send_sem=es_sem.at[d], recv_sem=e_sem.at[p_me],
-            device_id=plane_dev(to), device_id_type=MESH,
-        )
-
-    def send_err(d, carry):
-        err_copy(d).start()
-        return carry
-
-    lax.fori_loop(1, NP, send_err, 0)
+    def err_copy(dx, dg):
+        return pltpu.make_async_remote_copy(
+            src_ref=eout.at[g_to[dg]], dst_ref=ein.at[p_me],
+            send_sem=es_sem.at[dx * NG + dg], recv_sem=e_sem.at[p_me],
+            device_id=(gx_to[dx], g_to[dg]), device_id_type=MESH,
+        )
+
+    for dx, dg in plane:
+        err_copy(dx, dg).start()
     ein[p_me] = eout[g]
 
     q_store = pltpu.make_async_copy(qt, q_hbm, out_sem.at[0])
     q_store.start()
 
-    def err_got(d, carry):
-        other = lax.rem(p_me + d, NP)
+    def err_got(other):
         pltpu.make_async_remote_copy(
             src_ref=eout.at[0], dst_ref=ein.at[other],
             send_sem=es_sem.at[0], recv_sem=e_sem.at[other],
             device_id=(gx, g), device_id_type=MESH,
         ).wait_recv()
-        return carry
-
-    lax.fori_loop(1, NP, err_got, 0)
-
-    def sums(pp, total):
+
+    lax.fori_loop(0, NP // 2, places, 0)
+    total = jnp.zeros((NZ * 16, 128), F32)
+    for dx, dy in sorted(itertools.product(range(4), range(4)), key=lambda s: min(s[0], 4 - s[0]) + min(s[1], 4 - s[1])):
+        pp = lax.rem(x + dx, 4) * 4 + lax.rem(y_me + dy, 4)
+        if dx or dy:
+            err_got(2 * pp)
+            err_got(2 * pp + 1)
+        else:
+            err_got(2 * pp + 1 - core)
         for h in range(2):
             err = ein[2 * pp + h].astype(F32)
             owner = zrow[pp, 0:1, h * 128 : (h + 1) * 128]
@@ -350,16 +384,14 @@
                 lm[pp, a * 16 : (a + 1) * 16, h * 128 : (h + 1) * 128] = jnp.where(
                     owner == float(a), err, 0.0
                 ).astype(BF16)
-        return total + lax.dot_general(
+        total = total + lax.dot_general(
             lm[pp], bt[pp], (((1,), (1,)), ((), ())), preferred_element_type=F32
         )
-
-    total = jnp.zeros((NZ * 16, 128), F32)
-    for pp in range(NP // 2):
-        total = sums(pp, total)
     lane8 = lax.broadcasted_iota(jnp.int32, (8, 128), 1)
     for a in range(NZ):
-        pout[a] = jnp.where(lane8 < OWN, total[a * 16 : a * 16 + 8, :], total[a * 16 + 8 : a * 16 + 16, :])
+        pout[a] = jnp.where(
+            lane8 < OWN, total[a * 16 : a * 16 + 8, :], total[a * 16 + 8 : a * 16 + 16, :]
+        ).astype(BF16)
 
     def sum_copy(d):
         to = at_z(d)
@@ -379,7 +411,7 @@
             send_sem=ps_sem.at[0], recv_sem=p_sem.at[other],
             device_id=(gx, g), device_id_type=MESH,
         ).wait_recv()
-    whole = jnp.sum(pin[...], axis=0)
+    whole = jnp.sum(pin[...].astype(F32), axis=0)
     count = jnp.broadcast_to(whole[4:5, :], (8, 128))
     count = jnp.where(lane8 < OWN, pltpu.roll(count, OWN, 1), count)
     mean = whole / jnp.maximum(count, 1.0)
@@ -399,14 +431,12 @@
     lax.fori_loop(0, NZ, x_done, 0)
     for d in range(1, NG):
         book_copy(d).wait_send()
-        pick_copy(d).wait_send()
-
-    def plane_done(d, carry):
-        slot_copy(d).wait_send()
-        err_copy(d).wait_send()
-        return carry
-
-    lax.fori_loop(1, NP, plane_done, 0)
+    for k in (0, 2, 3, 4, 5, 6, 7):
+        pick_copy(0, k).wait_send()
+    for dx, dg in plane:
+        slot_copy(dx, dg).wait_send()
+        err_copy(dx, dg).wait_send()
+
     for d in range(1, NZ):
         sum_copy(d).wait_send()
     q_store.wait()
@@ -429,7 +459,8 @@
             pltpu.VMEM((1, 128), jnp.int32),
             pltpu.VMEM((32, 128), jnp.int32),
             pltpu.VMEM((32, 128), jnp.int32),
-            pltpu.VMEM((NZ * NX, OWN, FEAT), BF16),
+            pltpu.VMEM((OWN, FEAT), BF16),
+            pltpu.VMEM((NZ * NX, PACKED, 128), BF16),
             pltpu.VMEM((768, 768), BF16),
             pltpu.VMEM((NG, SUB, 8, CODES), BF16),
             pltpu.VMEM((2, 128), F32),
@@ -440,8 +471,8 @@
             pltpu.VMEM((NG // 2, SUB * CODES, 256), BF16),
             pltpu.VMEM((NG // 2, 256, 256), BF16),
             pltpu.VMEM((NG * ROWS, 128), F32),
-            pltpu.VMEM((NG, ROWS, FEAT), BF16),
-            pltpu.VMEM((NG, ROWS, FEAT), BF16),
+            pltpu.VMEM((NG, FEAT, 128), BF16),
+            pltpu.VMEM((NG, FEAT, 128), BF16),
             pltpu.VMEM((ROWS, 768), F32),
             pltpu.VMEM((NG, 16, ROWS), F32),
             pltpu.VMEM((768, ROWS), F32),
@@ -451,8 +482,8 @@
             pltpu.VMEM((NP // 2, 8, 256), F32),
             pltpu.VMEM((NP // 2, 128, 256), BF16),
             pltpu.VMEM((NP // 2, NZ * 16, 256), BF16),
-            pltpu.VMEM((NZ, 8, 128), F32),
-            pltpu.VMEM((NZ, 8, 128), F32),
+            pltpu.VMEM((NZ, 8, 128), BF16),
+            pltpu.VMEM((NZ, 8, 128), BF16),
             pltpu.VMEM((SUB, OWN), F32),
             dma((7,)),
             dma((NZ,)),
@@ -471,16 +502,21 @@
             dma((2,)),
         ],
         compiler_params=pltpu.CompilerParams(
-            collective_id=0, has_side_effects=True, vmem_limit_bytes=67043328
+            collective_id=0, has_side_effects=True, vmem_limit_bytes=48 * 1024 * 1024
         ),
     )(
-        vectors,
-        list_ids.reshape(1, ROWS),
-        old_order.reshape(32, 128),
-        new_order.reshape(32, 128),
-        centroids,
-        rotation,
-        codebook,
+        *(
+            pltpu.with_memory_space_constraint(one, pltpu.HBM)
+            for one in (
+                vectors,
+                list_ids.reshape(1, ROWS),
+                old_order.reshape(32, 128),
+                new_order.reshape(32, 128),
+                centroids,
+                rotation,
+                codebook,
+            )
+        )
     )
     return errors.T, means.T
 

time: 63 us -> 54.8 us (0.87); the launches traced: 61.8 us -> 54.6 us
  Pallas kernels: 58.4 us -> 52.7 us
  local copies, waits for them, and re-layouts: 2.72 us -> 1.22 us
    pallas_call x1, Pallas kernels: 58.4 us -> 52.7 us  [on_device(): pl.pallas_call(kernel, out_shape=(jax.ShapeDtypeStruct((NG * SUB, ROWS),...]
    unnamed x2, local copies, waits for them, and re-layouts: 2.72 us -> 1.22 us
where the time goes in v3:
time: 54.8 us; the launch traced here: 54.6 us
  Pallas kernels  52.7 us (96%)
  local copies, waits for them, and re-layouts  1.22 us (2%)
  between operations  0.64 us (1%)
    pallas_call x1, Pallas kernels, on_device(): pl.pallas_call(kernel, out_shape=(jax.ShapeDtypeStruct((NG * SUB, ROWS),...  52.7 us
    unnamed x2, local copies, waits for them, and re-layouts  1.22 us

profile of v3, /device:TPU:1, one launch (start us, length us, event | category | flops | bytes accessed | tf_op | source)
XLA Modules:
  0.0 54.6 jit_solution(4902482901650638070)
XLA Ops:
  0.6 52.7 %shard_map.86 = (f32[96,128]{1,0:T(8,128)S(1)}, f32[12,64]{1,0:T(8,128)S(1)}) custom-call(bf16[128,768]{1,0:T(8,128)(2,1)} %v_hbm.1, s32[1,128]{1,0:T(1,128)} %bitcast.9, s32[32,128]{1,0:T(8,128)} %bitcast.7, s32[32,128]{1,0:T(8,128)} %bitcast.8, bf16[64,96]{1,0:T(8,128)(2,1)} %c_hbm.1, bf16[768,768]{1,0:T(8,128)(2,1)} %r_hbm.1, bf16[12,8,256]{2,1,0:T(8,128)(2,1)} %cb_hbm.1), custom_call_target="tpu_custom_call" | custom-call | tf_op jit(solution)/shard_map/pallas_call | solution.py:449
  53.4 0.6 %copy.11 = f32[128,96]{0,1:T(8,128)} copy(f32[128,96]{0,1:T(8,128)S(1)} %bitcast.5) | data formatting | bytes 98304
  54.0 0.6 %copy.12 = f32[64,12]{0,1:T(8,128)} copy(f32[64,12]{0,1:T(8,128)S(1)} %bitcast.6) | data formatting | bytes 6144

commit v4 on v3

--- a/solution.py
+++ b/solution.py
@@ -1,5 +1,3 @@
-import itertools
-
 import jax
 import jax.numpy as jnp
 from jax import lax
@@ -23,17 +21,21 @@
 WIDE = 6
 HOP = 4
 NEAR = [4, -4, 1, -1, 2, -2, 3, -3]
+ARRIVAL = [
+    (0, 0), (0, 2), (0, 3), (1, 2), (3, 2), (1, 3), (3, 3), (0, 1),
+    (2, 2), (2, 3), (1, 1), (3, 1), (1, 0), (3, 0), (2, 1), (2, 0),
+]
 FAR = [5, -5, 6, -6, 7, -7, 8]
 
 
 def kernel(
     v_hbm, ids_hbm, old_hbm, new_hbm, c_hbm, r_hbm, cb_hbm,
-    q_hbm, le_hbm,
+    q_ref, mean_ref,
     v, ids, old, new, block_in, cg, rot, cb,
     slot_out, slots, high, low_hot, y, book, wt, acc, wout, win, vr,
-    qmin, tt, qt, eout, ein, zrow, bt, lm, pout, pin, lout,
+    qmin, tt, eout, ein, zrow, bt, lm, pout, pin,
     in_sem, zs_sem, xs_sem, ag_sem, cbs_sem, cb_sem, sls_sem, sl_sem,
-    ws_sem, w_sem, es_sem, e_sem, ps_sem, p_sem, out_sem,
+    ws_sem, w_sem, es_sem, e_sem, ps_sem, p_sem,
 ):
     gx, g = lax.axis_index("gx"), lax.axis_index("gy")
     z, x = gx // NX, gx % NX
@@ -46,6 +48,13 @@
     g_to = [lax.rem(g + d, NG) for d in range(NG)]
     gx_to = [z * NX + one for one in x_to]
     plane = [(dx, dg) for dx in (2, 1, 3, 0) for dg in (4, 5, 2, 3, 6, 7, 1, 0) if dx or dg]
+
+    barrier = pltpu.get_barrier_semaphore()
+    for off in NEAR:
+        pl.semaphore_signal(barrier, inc=1, device_id=(at_z(off) * NX + x, g), device_id_type=MESH)
+
+    for dx, dg in plane:
+        pl.semaphore_signal(barrier, inc=1, device_id=(gx_to[dx], g_to[dg]), device_id_type=MESH)
 
     loads = [
         pltpu.make_async_copy(c_hbm, block_in, in_sem.at[0]),
@@ -59,13 +68,6 @@
     for one in loads:
         one.start()
 
-    barrier = pltpu.get_barrier_semaphore()
-    for off in NEAR:
-        pl.semaphore_signal(barrier, inc=1, device_id=(at_z(off) * NX + x, g), device_id_type=MESH)
-
-    for dx, dg in plane:
-        pl.semaphore_signal(barrier, inc=1, device_id=(gx_to[dx], g_to[dg]), device_id_type=MESH)
-
     loads[0].wait()
     for k in range(3):
         tail = block_in[48:64, 32 * k : 32 * (k + 1)]
@@ -147,7 +149,7 @@
     vr[...] = jnp.dot(v[...], rot[...], preferred_element_type=F32)
 
     def spread(off):
-        for d in (1, 3, 2):
+        for d in (2, 1, 3):
             x_copy(at_z(off), d).start()
 
     for off in NEAR[2:6]:
@@ -265,15 +267,18 @@
         acc[...] = choose(part, offs, high[...], acc[...])
 
     order = [0, 1, -1, 2, -2, 3, -3, 4, -4] + FAR
+
+    def pass_on(offs):
+        for off in offs:
+            got(at_z(off) * NX + x)
+            spread(off)
+
     pick(order[0:2])
+    pass_on(FAR[0:2])
     pick(order[2:4])
-    for off in FAR[:4]:
-        got(at_z(off) * NX + x)
-        spread(off)
+    pass_on(FAR[2:4])
     pick(order[4:6])
-    for off in FAR[4:]:
-        got(at_z(off) * NX + x)
-        spread(off)
+    pass_on(FAR[4:])
     pick(order[6:8])
     for d in range(1, NG):
         book_got(d)
@@ -310,56 +315,61 @@
     win[g] = wout[g]
 
     lax.fori_loop(NG // 4, NG // 2, build_book, 0)
-    come = [g, 2 * y_me + 1 - core]
-    for dy in (1, 3, 2):
-        come += [2 * lax.rem(y_me + dy, NG // 2) + c for c in range(2)]
-    for k, other in enumerate(come):
-        if k:
-            pltpu.make_async_remote_copy(
-                src_ref=wout.at[0], dst_ref=win.at[other],
-                send_sem=ws_sem.at[0], recv_sem=w_sem.at[other],
-                device_id=(gx, g), device_id_type=MESH,
-            ).wait_recv()
-        packed = win[other]
-        tail = jnp.concatenate([packed[32 * k : 32 * (k + 1), FEAT:] for k in range(3)], axis=1)
-        rows = jnp.concatenate([packed[:, :FEAT], tail], axis=0)
-        vr[...] += jnp.dot(
-            rows, rot[pl.ds(pl.multiple_of(other * FEAT, 32), FEAT), :], preferred_element_type=F32
-        )
+    chips = [[2 * lax.rem(y_me + dy, NG // 2) + c for c in range(2)] for dy in (1, 3, 2)]
+    for group in ([g, 2 * y_me + 1 - core], chips[0], chips[1] + chips[2]):
+        for other in group:
+            if other is not g:
+                pltpu.make_async_remote_copy(
+                    src_ref=wout.at[0], dst_ref=win.at[other],
+                    send_sem=ws_sem.at[0], recv_sem=w_sem.at[other],
+                    device_id=(gx, g), device_id_type=MESH,
+                ).wait_recv()
+        moved = None
+        for other in group:
+            packed = win[other]
+            tail = jnp.concatenate([packed[32 * k : 32 * (k + 1), FEAT:] for k in range(3)], axis=1)
+            rows = jnp.concatenate([packed[:, :FEAT], tail], axis=0)
+            part = jnp.dot(
+                rows, rot[pl.ds(pl.multiple_of(other * FEAT, 32), FEAT), :], preferred_element_type=F32
+            )
+            moved = part if moved is None else moved + part
+        vr[...] += moved
     tt[...] = vr[...].T
     for j in range(NG):
         q, h = j // 2, j % 2
         part = tt[j * FEAT : (j + 1) * FEAT, :]
         wt[q, h * 128 : h * 128 + FEAT, h * 128 : (h + 1) * 128] = part.astype(BF16)
-        qt[j * SUB : (j + 1) * SUB, :] = jnp.sum((part * part).reshape(SUB, 8, ROWS), axis=1)
-
-    for q in range(NG // 2):
+        qmin[j, 0:SUB, :] = jnp.sum((part * part).reshape(SUB, 8, ROWS), axis=1)
+
+    def err_copy(dx, to, k):
+        return pltpu.make_async_remote_copy(
+            src_ref=eout.at[to], dst_ref=ein.at[p_me],
+            send_sem=es_sem.at[k], recv_sem=e_sem.at[p_me],
+            device_id=(gx_to[dx], to), device_id_type=MESH,
+        )
+
+    spare = jnp.ones((4, ROWS), F32)
+    err_sent = []
+    for dy in (2, 1, 3, 0):
+        q = lax.rem(y_me + dy, NG // 2)
         for i in range(0, SUB, WIDE):
             dist = jnp.dot(
                 book[q, i * CODES : (i + WIDE) * CODES, :], wt[q], preferred_element_type=F32
             )
             low = jnp.min(dist.reshape(WIDE, CODES, 256), axis=1)
-            qmin[2 * q, i : i + WIDE, :] = low[:, :128]
-            qmin[2 * q + 1, i : i + WIDE, :] = low[:, 128:]
+            qmin[2 * q, i : i + WIDE, :] += low[:, :128]
+            qmin[2 * q + 1, i : i + WIDE, :] += low[:, 128:]
+        for c in range(2):
+            eout[2 * q + c] = jnp.concatenate([qmin[2 * q + c, 0:SUB, :], spare], axis=0).astype(BF16)
+        for dx in (2, 1, 3, 0):
+            for c in range(2) if dx or dy else (0,):
+                to = 2 * q + c if dx or dy else 2 * q + 1 - core
+                err_sent.append(err_copy(dx, to, len(err_sent)))
+                err_sent[-1].start()
+    ein[p_me] = eout[g]
 
     for j in range(NG):
-        err = qt[j * SUB : (j + 1) * SUB, :] + qmin[j, 0:SUB, :]
-        qt[j * SUB : (j + 1) * SUB, :] = err
-        eout[j] = jnp.concatenate([err, jnp.ones((4, ROWS), F32)], axis=0).astype(BF16)
-
-    def err_copy(dx, dg):
-        return pltpu.make_async_remote_copy(
-            src_ref=eout.at[g_to[dg]], dst_ref=ein.at[p_me],
-            send_sem=es_sem.at[dx * NG + dg], recv_sem=e_sem.at[p_me],
-            device_id=(gx_to[dx], g_to[dg]), device_id_type=MESH,
-        )
-
-    for dx, dg in plane:
-        err_copy(dx, dg).start()
-    ein[p_me] = eout[g]
-
-    q_store = pltpu.make_async_copy(qt, q_hbm, out_sem.at[0])
-    q_store.start()
+        q_ref[j * SUB : (j + 1) * SUB, :] = qmin[j, 0:SUB, :]
 
     def err_got(other):
         pltpu.make_async_remote_copy(
@@ -370,7 +380,7 @@
 
     lax.fori_loop(0, NP // 2, places, 0)
     total = jnp.zeros((NZ * 16, 128), F32)
-    for dx, dy in sorted(itertools.product(range(4), range(4)), key=lambda s: min(s[0], 4 - s[0]) + min(s[1], 4 - s[1])):
+    for dx, dy in ARRIVAL:
         pp = lax.rem(x + dx, 4) * 4 + lax.rem(y_me + dy, 4)
         if dx or dy:
             err_got(2 * pp)
@@ -401,9 +411,25 @@
             device_id=(to * NX + x, g), device_id_type=MESH,
         )
 
-    for d in range(1, NZ):
+    for d in (8, 7, 9, 6, 10, 5, 11, 4, 12, 3, 13, 2, 14, 1, 15):
         sum_copy(d).start()
     pin[z] = pout[z]
+    for one in sent + err_sent:
+        one.wait_send()
+
+    def x_done(bz, carry):
+        for d in range(1, NX):
+            x_copy(bz, d).wait_send()
+        return carry
+
+    lax.fori_loop(0, NZ, x_done, 0)
+    for d in range(1, NG):
+        book_copy(d).wait_send()
+    for k in (0, 2, 3, 4, 5, 6, 7):
+        pick_copy(0, k).wait_send()
+    for dx, dg in plane:
+        slot_copy(dx, dg).wait_send()
+
     for d in range(1, NZ):
         other = at_z(d)
         pltpu.make_async_remote_copy(
@@ -415,32 +441,11 @@
     count = jnp.broadcast_to(whole[4:5, :], (8, 128))
     count = jnp.where(lane8 < OWN, pltpu.roll(count, OWN, 1), count)
     mean = whole / jnp.maximum(count, 1.0)
-    lout[0:8, :] = mean[:, :OWN]
-    lout[8:SUB, :] = pltpu.roll(mean, OWN, 1)[: SUB - 8, :OWN]
-    l_store = pltpu.make_async_copy(lout, le_hbm, out_sem.at[1])
-    l_store.start()
-
-    for one in sent:
-        one.wait_send()
-
-    def x_done(bz, carry):
-        for d in range(1, NX):
-            x_copy(bz, d).wait_send()
-        return carry
-
-    lax.fori_loop(0, NZ, x_done, 0)
-    for d in range(1, NG):
-        book_copy(d).wait_send()
-    for k in (0, 2, 3, 4, 5, 6, 7):
-        pick_copy(0, k).wait_send()
-    for dx, dg in plane:
-        slot_copy(dx, dg).wait_send()
-        err_copy(dx, dg).wait_send()
+    mean_ref[0:8, :] = mean[:, :OWN]
+    mean_ref[8:SUB, :] = pltpu.roll(mean, OWN, 1)[: SUB - 8, :OWN]
 
     for d in range(1, NZ):
         sum_copy(d).wait_send()
-    q_store.wait()
-    l_store.wait()
 
 
 def on_device(vectors, list_ids, old_order, new_order, centroids, rotation, codebook):
@@ -453,7 +458,7 @@
             jax.ShapeDtypeStruct((SUB, OWN), F32),
         ),
         in_specs=[any_spec] * 7,
-        out_specs=(any_spec, any_spec),
+        out_specs=(pl.BlockSpec(memory_space=pltpu.VMEM),) * 2,
         scratch_shapes=[
             pltpu.VMEM((ROWS, 768), BF16),
             pltpu.VMEM((1, 128), jnp.int32),
@@ -476,7 +481,6 @@
             pltpu.VMEM((ROWS, 768), F32),
             pltpu.VMEM((NG, 16, ROWS), F32),
             pltpu.VMEM((768, ROWS), F32),
-            pltpu.VMEM((NG * SUB, ROWS), F32),
             pltpu.VMEM((NG, 16, ROWS), BF16),
             pltpu.VMEM((NP, 16, ROWS), BF16),
             pltpu.VMEM((NP // 2, 8, 256), F32),
@@ -484,7 +488,6 @@
             pltpu.VMEM((NP // 2, NZ * 16, 256), BF16),
             pltpu.VMEM((NZ, 8, 128), BF16),
             pltpu.VMEM((NZ, 8, 128), BF16),
-            pltpu.VMEM((SUB, OWN), F32),
             dma((7,)),
             dma((NZ,)),
             dma((NZ * NX,)),
@@ -499,7 +502,6 @@
             dma((NP,)),
             dma((NZ,)),
             dma((NZ,)),
-            dma((2,)),
         ],
         compiler_params=pltpu.CompilerParams(
             collective_id=0, has_side_effects=True, vmem_limit_bytes=48 * 1024 * 1024

time: 54.8 us -> 53.6 us (0.978)
  Pallas kernels: 52.7 us -> 51.6 us
    pallas_call x1, Pallas kernels: 52.7 us -> 51.6 us  [on_device(): pl.pallas_call(kernel, out_shape=(jax.ShapeDtypeStruct((NG * SUB, ROWS),...]
where the time goes in v4:
time: 53.6 us; the launch traced here: 53.5 us
  Pallas kernels  51.6 us (96%)
  local copies, waits for them, and re-layouts  1.22 us (2%)
  between operations  0.64 us (1%)
    pallas_call x1, Pallas kernels, on_device(): pl.pallas_call(kernel, out_shape=(jax.ShapeDtypeStruct((NG * SUB, ROWS),...  51.6 us
    unnamed x2, local copies, waits for them, and re-layouts  1.22 us

profile of v4, /device:TPU:1, one launch (start us, length us, event | category | flops | bytes accessed | tf_op | source)
XLA Modules:
  0.0 53.5 jit_solution(17533107855857080688)
XLA Ops:
  0.6 51.6 %shard_map.86 = (f32[96,128]{1,0:T(8,128)S(1)}, f32[12,64]{1,0:T(8,128)S(1)}) custom-call(bf16[128,768]{1,0:T(8,128)(2,1)} %v_hbm.1, s32[1,128]{1,0:T(1,128)} %bitcast.9, s32[32,128]{1,0:T(8,128)} %bitcast.7, s32[32,128]{1,0:T(8,128)} %bitcast.8, bf16[64,96]{1,0:T(8,128)(2,1)} %c_hbm.1, bf16[768,768]{1,0:T(8,128)(2,1)} %r_hbm.1, bf16[12,8,256]{2,1,0:T(8,128)(2,1)} %cb_hbm.1), custom_call_target="tpu_custom_call" | custom-call | tf_op jit(solution)/shard_map/pallas_call | solution.py:454
  52.2 0.6 %copy.11 = f32[128,96]{0,1:T(8,128)} copy(f32[128,96]{0,1:T(8,128)S(1)} %bitcast.5) | data formatting | bytes 98304
  52.9 0.6 %copy.12 = f32[64,12]{0,1:T(8,128)} copy(f32[64,12]{0,1:T(8,128)S(1)} %bitcast.6) | data formatting | bytes 6144

commit v5 on v4

--- a/solution.py
+++ b/solution.py
@@ -26,6 +26,7 @@
     (2, 2), (2, 3), (1, 1), (3, 1), (1, 0), (3, 0), (2, 1), (2, 0),
 ]
 FAR = [5, -5, 6, -6, 7, -7, 8]
+ORDER = [0, 1, -1, 2, -2, 3, -3, 4, -4] + FAR
 
 
 def kernel(
@@ -34,7 +35,7 @@
     v, ids, old, new, block_in, cg, rot, cb,
     slot_out, slots, high, low_hot, y, book, wt, acc, wout, win, vr,
     qmin, tt, eout, ein, zrow, bt, lm, pout, pin,
-    in_sem, zs_sem, xs_sem, ag_sem, cbs_sem, cb_sem, sls_sem, sl_sem,
+    in_sem, zs_sem, xs_sem, ag_sem, ax_sem, cbs_sem, cb_sem, sls_sem, sl_sem,
     ws_sem, w_sem, es_sem, e_sem, ps_sem, p_sem,
 ):
     gx, g = lax.axis_index("gx"), lax.axis_index("gy")
@@ -76,35 +77,35 @@
         )
     pl.semaphore_wait(barrier, len(NEAR) + NP - 1)
 
-    def z_copy(block_z, to_off, k):
+    def all_of(ref, sem):
+        return pltpu.make_async_remote_copy(
+            src_ref=ref, dst_ref=ref, send_sem=sem, recv_sem=sem,
+            device_id=(gx, g), device_id_type=MESH,
+        )
+
+    def z_copy(block_z, to_off):
         block = block_z * NX + x
         return pltpu.make_async_remote_copy(
             src_ref=cg.at[block], dst_ref=cg.at[block],
-            send_sem=zs_sem.at[k], recv_sem=ag_sem.at[block],
+            send_sem=zs_sem, recv_sem=ag_sem.at[block_z],
             device_id=(at_z(to_off) * NX + x, g), device_id_type=MESH,
         )
 
-    def x_copy(block_z, d):
-        block = block_z * NX + x
+    def x_copy(off, d):
+        block = at_z(off) * NX + x
         return pltpu.make_async_remote_copy(
             src_ref=cg.at[block], dst_ref=cg.at[block],
-            send_sem=xs_sem.at[block_z * NX + d], recv_sem=ag_sem.at[block],
-            device_id=(z * NX + lax.rem(x + d, NX), g), device_id_type=MESH,
-        )
-
-    def got(block):
-        pltpu.make_async_remote_copy(
-            src_ref=cg.at[block], dst_ref=cg.at[block],
-            send_sem=zs_sem.at[0], recv_sem=ag_sem.at[block],
-            device_id=(gx, g), device_id_type=MESH,
-        ).wait_recv()
-
-    sent = []
-    for k, off in enumerate(NEAR):
-        sent.append(z_copy(z, off, k))
-        sent[-1].start()
+            send_sem=xs_sem, recv_sem=ax_sem.at[ORDER.index(off) // 2],
+            device_id=(gx_to[d], g), device_id_type=MESH,
+        )
+
+    def got(off):
+        all_of(cg.at[0], ag_sem.at[at_z(off)]).wait_recv()
+
+    for off in NEAR:
+        z_copy(z, off).start()
     for d in (1, 3, 2):
-        x_copy(z, d).start()
+        x_copy(0, d).start()
 
     for k in (1, 2, 3):
         loads[k].wait()
@@ -125,7 +126,7 @@
     def slot_copy(dx, dg):
         return pltpu.make_async_remote_copy(
             src_ref=slot_out, dst_ref=slots.at[p_me],
-            send_sem=sls_sem.at[dx * NG + dg], recv_sem=sl_sem.at[p_me],
+            send_sem=sls_sem, recv_sem=sl_sem,
             device_id=(gx_to[dx], g_to[dg]), device_id_type=MESH,
         )
 
@@ -136,7 +137,7 @@
     def book_copy(d):
         return pltpu.make_async_remote_copy(
             src_ref=cb.at[g], dst_ref=cb.at[g],
-            send_sem=cbs_sem.at[d], recv_sem=cb_sem.at[g],
+            send_sem=cbs_sem, recv_sem=cb_sem,
             device_id=(gx, lax.rem(g + d, NG)), device_id_type=MESH,
         )
 
@@ -150,22 +151,19 @@
 
     def spread(off):
         for d in (2, 1, 3):
-            x_copy(at_z(off), d).start()
+            x_copy(off, d).start()
 
     for off in NEAR[2:6]:
-        got(at_z(off) * NX + x)
+        got(off)
         spread(off)
-    k = len(NEAR)
     for off in NEAR[:2]:
-        got(at_z(off) * NX + x)
+        got(off)
         step = -1 if off > 0 else 1
         for far in range(HOP if off > 0 else HOP - 1, 0, -1):
-            sent.append(z_copy(at_z(off), step * far, k))
-            sent[-1].start()
-            k += 1
+            z_copy(at_z(off), step * far).start()
     for off in NEAR[6:] + NEAR[:2]:
         if abs(off) < HOP:
-            got(at_z(off) * NX + x)
+            got(off)
         spread(off)
 
     y[...] = jnp.zeros_like(y)
@@ -173,14 +171,6 @@
     for q in range(NG // 2):
         for h in range(2):
             wt[q, h * 128 + FEAT : (h + 1) * 128, h * 128 : (h + 1) * 128] = jnp.ones((32, 128), BF16)
-
-    def book_got(d):
-        other = lax.rem(g + d, NG)
-        pltpu.make_async_remote_copy(
-            src_ref=cb.at[other], dst_ref=cb.at[other],
-            send_sem=cbs_sem.at[0], recv_sem=cb_sem.at[other],
-            device_id=(gx, g), device_id_type=MESH,
-        ).wait_recv()
 
     lane_row = lax.broadcasted_iota(jnp.int32, (1, 128), 1)
     member = jnp.where(lane_row < FEAT, lane_row // 8, lax.rem(lane_row - FEAT, 16))
@@ -200,16 +190,7 @@
         return carry
 
 
-    def slot_got(d, carry):
-        other = lax.rem(p_me + d, NP)
-        pltpu.make_async_remote_copy(
-            src_ref=slot_out, dst_ref=slots.at[other],
-            send_sem=sls_sem.at[0], recv_sem=sl_sem.at[other],
-            device_id=(gx, g), device_id_type=MESH,
-        ).wait_recv()
-        return carry
-
-    lax.fori_loop(1, NP, slot_got, 0)
+    all_of(slots.at[0 : NP - 1], sl_sem).wait_recv()
 
     def columns(j, carry):
         row = slots[x * NG + j][0:1, :].astype(jnp.int32)
@@ -243,11 +224,10 @@
     blank = jnp.zeros((16, 128 - FEAT), BF16)
 
     def operand(offs):
+        all_of(cg.at[0:6], ax_sem.at[ORDER.index(offs[0]) // 2]).wait_recv()
         sides = []
         for off in offs:
             cz = at_z(off)
-            for d in (1, 3, 2):
-                got(cz * NX + lax.rem(x + d, NX))
             blocks = [cg[cz * NX + b] for b in range(NX)]
             tails = [
                 jnp.concatenate(
@@ -266,34 +246,32 @@
         part = jnp.dot(low_hot[...], operand(offs), preferred_element_type=F32)
         acc[...] = choose(part, offs, high[...], acc[...])
 
-    order = [0, 1, -1, 2, -2, 3, -3, 4, -4] + FAR
 
     def pass_on(offs):
         for off in offs:
-            got(at_z(off) * NX + x)
+            got(off)
             spread(off)
 
-    pick(order[0:2])
+    pick(ORDER[0:2])
     pass_on(FAR[0:2])
-    pick(order[2:4])
+    pick(ORDER[2:4])
     pass_on(FAR[2:4])
-    pick(order[4:6])
+    pick(ORDER[4:6])
     pass_on(FAR[4:])
-    pick(order[6:8])
-    for d in range(1, NG):
-        book_got(d)
+    pick(ORDER[6:8])
+    all_of(cb.at[0 : NG - 1], cb_sem).wait_recv()
     lax.fori_loop(0, NG // 4, build_book, 0)
     for k in range(NZ // 2, NZ - 2, 2):
-        pick(order[k : k + 2])
-
-    def pick_copy(to, k):
+        pick(ORDER[k : k + 2])
+
+    def pick_copy(to):
         return pltpu.make_async_remote_copy(
             src_ref=wout.at[to], dst_ref=win.at[g],
-            send_sem=ws_sem.at[k], recv_sem=w_sem.at[g],
+            send_sem=ws_sem, recv_sem=w_sem.at[g // 2],
             device_id=(gx, to), device_id_type=MESH,
         )
 
-    last = order[NZ - 2 :]
+    last = ORDER[NZ - 2 :]
     final = operand(last)
     y_me, core = g // 2, g % 2
     for dy in (2, 1, 3, 0):
@@ -309,21 +287,16 @@
                 )
         if dy:
             for c in range(2):
-                pick_copy(2 * chip + c, 2 * dy + c).start()
+                pick_copy(2 * chip + c).start()
         else:
-            pick_copy(2 * chip + 1 - core, 0).start()
+            pick_copy(2 * chip + 1 - core).start()
     win[g] = wout[g]
 
     lax.fori_loop(NG // 4, NG // 2, build_book, 0)
     chips = [[2 * lax.rem(y_me + dy, NG // 2) + c for c in range(2)] for dy in (1, 3, 2)]
-    for group in ([g, 2 * y_me + 1 - core], chips[0], chips[1] + chips[2]):
-        for other in group:
-            if other is not g:
-                pltpu.make_async_remote_copy(
-                    src_ref=wout.at[0], dst_ref=win.at[other],
-                    send_sem=ws_sem.at[0], recv_sem=w_sem.at[other],
-                    device_id=(gx, g), device_id_type=MESH,
-                ).wait_recv()
+    for dys, group in (((0,), [g, 2 * y_me + 1 - core]), ((1,), chips[0]), ((3, 2), chips[1] + chips[2])):
+        for dy in dys:
+            all_of(win.at[0 : 2 if dy else 1], w_sem.at[lax.rem(y_me + dy, NG // 2)]).wait_recv()
         moved = None
         for other in group:
             packed = win[other]
@@ -341,15 +314,14 @@
         wt[q, h * 128 : h * 128 + FEAT, h * 128 : (h + 1) * 128] = part.astype(BF16)
         qmin[j, 0:SUB, :] = jnp.sum((part * part).reshape(SUB, 8, ROWS), axis=1)
 
-    def err_copy(dx, to, k):
+    def err_copy(dx, to):
         return pltpu.make_async_remote_copy(
             src_ref=eout.at[to], dst_ref=ein.at[p_me],
-            send_sem=es_sem.at[k], recv_sem=e_sem.at[p_me],
+            send_sem=es_sem, recv_sem=e_sem.at[p_me // 2],
             device_id=(gx_to[dx], to), device_id_type=MESH,
         )
 
     spare = jnp.ones((4, ROWS), F32)
-    err_sent = []
     for dy in (2, 1, 3, 0):
         q = lax.rem(y_me + dy, NG // 2)
         for i in range(0, SUB, WIDE):
@@ -364,29 +336,17 @@
         for dx in (2, 1, 3, 0):
             for c in range(2) if dx or dy else (0,):
                 to = 2 * q + c if dx or dy else 2 * q + 1 - core
-                err_sent.append(err_copy(dx, to, len(err_sent)))
-                err_sent[-1].start()
+                err_copy(dx, to).start()
     ein[p_me] = eout[g]
 
     for j in range(NG):
         q_ref[j * SUB : (j + 1) * SUB, :] = qmin[j, 0:SUB, :]
-
-    def err_got(other):
-        pltpu.make_async_remote_copy(
-            src_ref=eout.at[0], dst_ref=ein.at[other],
-            send_sem=es_sem.at[0], recv_sem=e_sem.at[other],
-            device_id=(gx, g), device_id_type=MESH,
-        ).wait_recv()
 
     lax.fori_loop(0, NP // 2, places, 0)
     total = jnp.zeros((NZ * 16, 128), F32)
     for dx, dy in ARRIVAL:
         pp = lax.rem(x + dx, 4) * 4 + lax.rem(y_me + dy, 4)
-        if dx or dy:
-            err_got(2 * pp)
-            err_got(2 * pp + 1)
-        else:
-            err_got(2 * pp + 1 - core)
+        all_of(ein.at[0 : 2 if dx or dy else 1], e_sem.at[pp]).wait_recv()
         for h in range(2):
             err = ein[2 * pp + h].astype(F32)
             owner = zrow[pp, 0:1, h * 128 : (h + 1) * 128]
@@ -407,36 +367,24 @@
         to = at_z(d)
         return pltpu.make_async_remote_copy(
             src_ref=pout.at[to], dst_ref=pin.at[z],
-            send_sem=ps_sem.at[d], recv_sem=p_sem.at[z],
+            send_sem=ps_sem, recv_sem=p_sem,
             device_id=(to * NX + x, g), device_id_type=MESH,
         )
 
     for d in (8, 7, 9, 6, 10, 5, 11, 4, 12, 3, 13, 2, 14, 1, 15):
         sum_copy(d).start()
     pin[z] = pout[z]
-    for one in sent + err_sent:
-        one.wait_send()
-
-    def x_done(bz, carry):
-        for d in range(1, NX):
-            x_copy(bz, d).wait_send()
-        return carry
-
-    lax.fori_loop(0, NZ, x_done, 0)
-    for d in range(1, NG):
-        book_copy(d).wait_send()
-    for k in (0, 2, 3, 4, 5, 6, 7):
-        pick_copy(0, k).wait_send()
-    for dx, dg in plane:
-        slot_copy(dx, dg).wait_send()
-
-    for d in range(1, NZ):
-        other = at_z(d)
-        pltpu.make_async_remote_copy(
-            src_ref=pout.at[0], dst_ref=pin.at[other],
-            send_sem=ps_sem.at[0], recv_sem=p_sem.at[other],
-            device_id=(gx, g), device_id_type=MESH,
-        ).wait_recv()
+    for ref, sem in (
+        (cg.at[0 : NZ - 1], zs_sem),
+        (cg.at[0 : NZ * (NX - 1)], xs_sem),
+        (cb.at[0 : NG - 1], cbs_sem),
+        (slots.at[0 : NP - 1], sls_sem),
+        (wout.at[0 : NG - 1], ws_sem),
+        (ein.at[0 : NP - 1], es_sem),
+    ):
+        all_of(ref, sem).wait_send()
+
+    all_of(pin.at[0 : NZ - 1], p_sem).wait_recv()
     whole = jnp.sum(pin[...].astype(F32), axis=0)
     count = jnp.broadcast_to(whole[4:5, :], (8, 128))
     count = jnp.where(lane8 < OWN, pltpu.roll(count, OWN, 1), count)
@@ -444,8 +392,7 @@
     mean_ref[0:8, :] = mean[:, :OWN]
     mean_ref[8:SUB, :] = pltpu.roll(mean, OWN, 1)[: SUB - 8, :OWN]
 
-    for d in range(1, NZ):
-        sum_copy(d).wait_send()
+    all_of(pout.at[0 : NZ - 1], ps_sem).wait_send()
 
 
 def on_device(vectors, list_ids, old_order, new_order, centroids, rotation, codebook):
@@ -489,19 +436,20 @@
             pltpu.VMEM((NZ, 8, 128), BF16),
             pltpu.VMEM((NZ, 8, 128), BF16),
             dma((7,)),
+            dma,
+            dma,
             dma((NZ,)),
-            dma((NZ * NX,)),
-            dma((NZ * NX,)),
-            dma((NG,)),
-            dma((NG,)),
-            dma((NP,)),
-            dma((NP,)),
-            dma((NG,)),
-            dma((NG,)),
-            dma((NP,)),
-            dma((NP,)),
-            dma((NZ,)),
-            dma((NZ,)),
+            dma((NZ // 2,)),
+            dma,
+            dma,
+            dma,
+            dma,
+            dma,
+            dma((NG // 2,)),
+            dma,
+            dma((NP // 2,)),
+            dma,
+            dma,
         ],
         compiler_params=pltpu.CompilerParams(
             collective_id=0, has_side_effects=True, vmem_limit_bytes=48 * 1024 * 1024

time: 53.6 us -> 50.9 us (0.950)
  Pallas kernels: 51.6 us -> 48.9 us
    pallas_call x1, Pallas kernels: 51.6 us -> 48.9 us  [on_device(): pl.pallas_call(kernel, out_shape=(jax.ShapeDtypeStruct((NG * SUB, ROWS),...]
where the time goes in v5:
time: 50.9 us; the launch traced here: 50.7 us
  Pallas kernels  48.9 us (96%)
  local copies, waits for them, and re-layouts  1.22 us (2%)
  between operations  0.64 us (1%)
    pallas_call x1, Pallas kernels, on_device(): pl.pallas_call(kernel, out_shape=(jax.ShapeDtypeStruct((NG * SUB, ROWS),...  48.9 us
    unnamed x2, local copies, waits for them, and re-layouts  1.22 us

profile of v5, /device:TPU:1, one launch (start us, length us, event | category | flops | bytes accessed | tf_op | source)
XLA Modules:
  0.0 50.7 jit_solution(7922264442207490968)
XLA Ops:
  0.6 48.9 %shard_map.86 = (f32[96,128]{1,0:T(8,128)S(1)}, f32[12,64]{1,0:T(8,128)S(1)}) custom-call(bf16[128,768]{1,0:T(8,128)(2,1)} %v_hbm.1, s32[1,128]{1,0:T(1,128)} %bitcast.9, s32[32,128]{1,0:T(8,128)} %bitcast.7, s32[32,128]{1,0:T(8,128)} %bitcast.8, bf16[64,96]{1,0:T(8,128)(2,1)} %c_hbm.1, bf16[768,768]{1,0:T(8,128)(2,1)} %r_hbm.1, bf16[12,8,256]{2,1,0:T(8,128)(2,1)} %cb_hbm.1), custom_call_target="tpu_custom_call" | custom-call | tf_op jit(solution)/shard_map/pallas_call | solution.py:401
  49.5 0.6 %copy.11 = f32[128,96]{0,1:T(8,128)} copy(f32[128,96]{0,1:T(8,128)S(1)} %bitcast.5) | data formatting | bytes 98304
  50.1 0.6 %copy.12 = f32[64,12]{0,1:T(8,128)} copy(f32[64,12]{0,1:T(8,128)S(1)} %bitcast.6) | data formatting | bytes 6144

commit v6 on v5

--- a/solution.py
+++ b/solution.py
@@ -159,7 +159,7 @@
     for off in NEAR[:2]:
         got(off)
         step = -1 if off > 0 else 1
-        for far in range(HOP if off > 0 else HOP - 1, 0, -1):
+        for far in (1, 4, 3, 2) if off > 0 else (1, 3, 2):
             z_copy(at_z(off), step * far).start()
     for off in NEAR[6:] + NEAR[:2]:
         if abs(off) < HOP:
@@ -293,17 +293,21 @@
     win[g] = wout[g]
 
     lax.fori_loop(NG // 4, NG // 2, build_book, 0)
-    chips = [[2 * lax.rem(y_me + dy, NG // 2) + c for c in range(2)] for dy in (1, 3, 2)]
-    for dys, group in (((0,), [g, 2 * y_me + 1 - core]), ((1,), chips[0]), ((3, 2), chips[1] + chips[2])):
-        for dy in dys:
-            all_of(win.at[0 : 2 if dy else 1], w_sem.at[lax.rem(y_me + dy, NG // 2)]).wait_recv()
+    for dys in ((0,), (1,), (3, 2)):
+        chips = [lax.rem(y_me + dy, NG // 2) for dy in dys]
+        for dy, chip in zip(dys, chips):
+            all_of(win.at[0 : 2 if dy else 1], w_sem.at[chip]).wait_recv()
         moved = None
-        for other in group:
-            packed = win[other]
-            tail = jnp.concatenate([packed[32 * k : 32 * (k + 1), FEAT:] for k in range(3)], axis=1)
-            rows = jnp.concatenate([packed[:, :FEAT], tail], axis=0)
+        for chip in chips:
+            sides = []
+            for c in range(2):
+                packed = win[2 * chip + c]
+                tail = jnp.concatenate([packed[32 * k : 32 * (k + 1), FEAT:] for k in range(3)], axis=1)
+                sides.append(jnp.concatenate([packed[:, :FEAT], tail], axis=0))
             part = jnp.dot(
-                rows, rot[pl.ds(pl.multiple_of(other * FEAT, 32), FEAT), :], preferred_element_type=F32
+                jnp.concatenate(sides, axis=1),
+                rot[pl.ds(pl.multiple_of(chip * 2 * FEAT, 64), 2 * FEAT), :],
+                preferred_element_type=F32,
             )
             moved = part if moved is None else moved + part
         vr[...] += moved
@@ -395,10 +399,21 @@
     all_of(pout.at[0 : NZ - 1], ps_sem).wait_send()
 
 
+def put_out(q_in, mean_in, q_out, mean_out, q_sem, mean_sem):
+    copies = [
+        pltpu.make_async_copy(q_in, q_out, q_sem),
+        pltpu.make_async_copy(mean_in, mean_out, mean_sem),
+    ]
+    for one in copies:
+        one.start()
+    for one in copies:
+        one.wait()
+
+
 def on_device(vectors, list_ids, old_order, new_order, centroids, rotation, codebook):
     dma = pltpu.SemaphoreType.DMA
     any_spec = pl.BlockSpec(memory_space=pltpu.HBM)
-    errors, means = pl.pallas_call(
+    found = pl.pallas_call(
         kernel,
         out_shape=(
             jax.ShapeDtypeStruct((NG * SUB, ROWS), F32),
@@ -468,6 +483,16 @@
             )
         )
     )
+    errors, means = pl.pallas_call(
+        put_out,
+        out_shape=(
+            jax.ShapeDtypeStruct((NG * SUB, ROWS), F32),
+            jax.ShapeDtypeStruct((SUB, OWN), F32),
+        ),
+        in_specs=[pl.BlockSpec(memory_space=pltpu.VMEM)] * 2,
+        out_specs=(any_spec, any_spec),
+        scratch_shapes=[dma, dma],
+    )(*(pltpu.with_memory_space_constraint(one, pltpu.VMEM) for one in found))
     return errors.T, means.T
 
 

time: 50.9 us -> 50.2 us (0.986)
  local copies, waits for them, and re-layouts: 1.22 us -> 0 us
    unnamed x2 -> x0, local copies, waits for them, and re-layouts: 1.22 us -> none
    pallas_call x0 -> x1, Pallas kernels: none -> 0.64 us  [on_device(): pl.pallas_call(put_out, out_shape=(jax.ShapeDtypeStruct((NG * SUB, ROWS),...]
where the time goes in v6:
time: 50.2 us; the launch traced here: 50 us
  Pallas kernels  49.4 us (98%)
  between operations  0.64 us (1%)
    pallas_call x1, Pallas kernels, on_device(): pl.pallas_call(kernel, out_shape=(jax.ShapeDtypeStruct((NG * SUB, ROWS),...  48.7 us

profile of v6, /device:TPU:1, one launch (start us, length us, event | category | flops | bytes accessed | tf_op | source)
XLA Modules:
  0.0 50.0 jit_solution(17446386483131651471)
XLA Ops:
  0.6 48.7 %shard_map.86 = (f32[96,128]{1,0:T(8,128)S(1)}, f32[12,64]{1,0:T(8,128)S(1)}) custom-call(bf16[128,768]{1,0:T(8,128)(2,1)} %v_hbm.1, s32[1,128]{1,0:T(1,128)} %bitcast.7, s32[32,128]{1,0:T(8,128)} %bitcast.5, s32[32,128]{1,0:T(8,128)} %bitcast.6, bf16[64,96]{1,0:T(8,128)(2,1)} %c_hbm.1, bf16[768,768]{1,0:T(8,128)(2,1)} %r_hbm.1, bf16[12,8,256]{2,1,0:T(8,128)(2,1)} %cb_hbm.1), custom_call_target="tpu_custom_call" | custom-call | tf_op jit(solution)/shard_map/pallas_call | solution.py:416
  49.4 0.6 %shard_map.87 = (f32[96,128]{1,0:T(8,128)}, f32[12,64]{1,0:T(8,128)}) custom-call(f32[96,128]{1,0:T(8,128)S(1)} %get-tuple-element.6.q_in, f32[12,64]{1,0:T(8,128)S(1)} %get-tuple-element.7.mean_in), custom_call_target="tpu_custom_call" | custom-call | tf_op jit(solution)/shard_map/pallas_call | solution.py:486

commit v7 on v6

--- a/solution.py
+++ b/solution.py
@@ -35,7 +35,7 @@
     v, ids, old, new, block_in, cg, rot, cb,
     slot_out, slots, high, low_hot, y, book, wt, acc, wout, win, vr,
     qmin, tt, eout, ein, zrow, bt, lm, pout, pin,
-    in_sem, zs_sem, xs_sem, ag_sem, ax_sem, cbs_sem, cb_sem, sls_sem, sl_sem,
+    in_sem, zs_sem, xs_sem, ag_sem, ax_sem, cbs_sem, cb_sem, sls_sem, sl_sem, slx_sem,
     ws_sem, w_sem, es_sem, e_sem, ps_sem, p_sem,
 ):
     gx, g = lax.axis_index("gx"), lax.axis_index("gy")
@@ -54,7 +54,8 @@
     for off in NEAR:
         pl.semaphore_signal(barrier, inc=1, device_id=(at_z(off) * NX + x, g), device_id_type=MESH)
 
-    for dx, dg in plane:
+    beside = [(dx, dg) for dx, dg in plane if dx == 0 or dg == 0]
+    for dx, dg in beside:
         pl.semaphore_signal(barrier, inc=1, device_id=(gx_to[dx], g_to[dg]), device_id_type=MESH)
 
     loads = [
@@ -75,7 +76,7 @@
         cg[gx, 16 * k : 16 * (k + 1), :] = jnp.concatenate(
             [block_in[16 * k : 16 * (k + 1), :], tail], axis=1
         )
-    pl.semaphore_wait(barrier, len(NEAR) + NP - 1)
+    pl.semaphore_wait(barrier, len(NEAR) + len(beside))
 
     def all_of(ref, sem):
         return pltpu.make_async_remote_copy(
@@ -126,12 +127,13 @@
     def slot_copy(dx, dg):
         return pltpu.make_async_remote_copy(
             src_ref=slot_out, dst_ref=slots.at[p_me],
-            send_sem=sls_sem, recv_sem=sl_sem,
+            send_sem=sls_sem, recv_sem=slx_sem if dx else sl_sem,
             device_id=(gx_to[dx], g_to[dg]), device_id_type=MESH,
         )
 
     for dx, dg in plane:
-        slot_copy(dx, dg).start()
+        if dx == 0:
+            slot_copy(dx, dg).start()
     slots[p_me] = slot_out[...]
 
     def book_copy(d):
@@ -190,7 +192,7 @@
         return carry
 
 
-    all_of(slots.at[0 : NP - 1], sl_sem).wait_recv()
+    all_of(slots.at[0 : NG - 1], sl_sem).wait_recv()
 
     def columns(j, carry):
         row = slots[x * NG + j][0:1, :].astype(jnp.int32)
@@ -253,6 +255,9 @@
             spread(off)
 
     pick(ORDER[0:2])
+    for dx, dg in plane:
+        if dx:
+            slot_copy(dx, dg).start()
     pass_on(FAR[0:2])
     pick(ORDER[2:4])
     pass_on(FAR[2:4])
@@ -346,6 +351,7 @@
     for j in range(NG):
         q_ref[j * SUB : (j + 1) * SUB, :] = qmin[j, 0:SUB, :]
 
+    all_of(slots.at[0 : NP - NG], slx_sem).wait_recv()
     lax.fori_loop(0, NP // 2, places, 0)
     total = jnp.zeros((NZ * 16, 128), F32)
     for dx, dy in ARRIVAL:
@@ -460,6 +466,7 @@
             dma,
             dma,
             dma,
+            dma,
             dma((NG // 2,)),
             dma,
             dma((NP // 2,)),

time: 50.2 us -> 48.7 us (0.970)
  Pallas kernels: 49.4 us -> 47.9 us
    pallas_call x1, Pallas kernels: 48.7 us -> 47.2 us  [on_device(): pl.pallas_call(kernel, out_shape=(jax.ShapeDtypeStruct((NG * SUB, ROWS),...]
where the time goes in v7:
time: 48.7 us; the launch traced here: 48.5 us
  Pallas kernels  47.9 us (98%)
  between operations  0.64 us (1%)
    pallas_call x1, Pallas kernels, on_device(): pl.pallas_call(kernel, out_shape=(jax.ShapeDtypeStruct((NG * SUB, ROWS),...  47.2 us

profile of v7, /device:TPU:1, one launch (start us, length us, event | category | flops | bytes accessed | tf_op | source)
XLA Modules:
  0.0 48.5 jit_solution(8657008932340473737)
XLA Ops:
  0.6 47.2 %shard_map.86 = (f32[96,128]{1,0:T(8,128)S(1)}, f32[12,64]{1,0:T(8,128)S(1)}) custom-call(bf16[128,768]{1,0:T(8,128)(2,1)} %v_hbm.1, s32[1,128]{1,0:T(1,128)} %bitcast.7, s32[32,128]{1,0:T(8,128)} %bitcast.5, s32[32,128]{1,0:T(8,128)} %bitcast.6, bf16[64,96]{1,0:T(8,128)(2,1)} %c_hbm.1, bf16[768,768]{1,0:T(8,128)(2,1)} %r_hbm.1, bf16[12,8,256]{2,1,0:T(8,128)(2,1)} %cb_hbm.1), custom_call_target="tpu_custom_call" | custom-call | tf_op jit(solution)/shard_map/pallas_call | solution.py:422
  47.9 0.6 %shard_map.87 = (f32[96,128]{1,0:T(8,128)}, f32[12,64]{1,0:T(8,128)}) custom-call(f32[96,128]{1,0:T(8,128)S(1)} %get-tuple-element.6.q_in, f32[12,64]{1,0:T(8,128)S(1)} %get-tuple-element.7.mean_in), custom_call_target="tpu_custom_call" | custom-call | tf_op jit(solution)/shard_map/pallas_call | solution.py:493
